TPU v7x, 32 devices: a whole 2x2x4 slice. The times are simulated.
32 devices in a mesh: rep: 4 (over x, y), dp: 8 (over z, core).
Axes of the slice: x: 2, y: 2, z: 4, core: 2. Of those that a mesh axis runs over, the one named last changes fastest.
Arguments:
- g_w_gate: bfloat16 [32, 2, 1152, 4608], P(('rep', 'dp')), parts along dimension 0
- g_w_up: bfloat16 [32, 2, 1152, 4608], P(('rep', 'dp')), parts along dimension 0
- g_w_down: bfloat16 [32, 2, 4608, 1152], P(('rep', 'dp')), parts along dimension 0
- w_gate: bfloat16 [2, 1152, 4608], replicated
- w_up: bfloat16 [2, 1152, 4608], replicated
- w_down: bfloat16 [2, 4608, 1152], replicated
- m_w_gate: float32 [2, 1152, 4608], P(None, 'dp')
- m_w_up: float32 [2, 1152, 4608], P(None, 'dp')
- m_w_down: float32 [2, 4608, 1152], P(None, 'dp')
- v_w_gate: float32 [2, 1152, 4608], P(None, 'dp')
- v_w_up: float32 [2, 1152, 4608], P(None, 'dp')
- v_w_down: float32 [2, 4608, 1152], P(None, 'dp')
Outputs:
- output 1: bfloat16 [8, 1152, 4608], P('rep'), parts along dimension 0
- output 2: bfloat16 [8, 1152, 4608], P('rep'), parts along dimension 0
- output 3: bfloat16 [8, 4608, 1152], P('rep'), parts along dimension 0
- output 4: float32 [8, 1152, 4608], P('rep', 'dp'), parts along dimension 0
- output 5: float32 [8, 1152, 4608], P('rep', 'dp'), parts along dimension 0
- output 6: float32 [8, 4608, 1152], P('rep', 'dp'), parts along dimension 0
- output 7: float32 [8, 1152, 4608], P('rep', 'dp'), parts along dimension 0
- output 8: float32 [8, 1152, 4608], P('rep', 'dp'), parts along dimension 0
- output 9: float32 [8, 4608, 1152], P('rep', 'dp'), parts along dimension 0
There are 4 independent parts. A program takes and returns all parts, laid end to end along the dimension named above; an argument that names none is the same for every part.
All inputs are finite; a program needn't handle non-finite values.
Results may differ from a plain program's by a relative error of at most 0.022.
Values are sent between devices in bfloat16 or wider.
A program may use at most 2 GiB of HBM per device.

v0:
```python
import functools

import jax
import jax.numpy as jnp
from jax import lax
from jax.experimental import pallas as pl
from jax.experimental.pallas import tpu as pltpu
from jax.sharding import PartitionSpec as P

MESH = pl.DeviceIdType.MESH
ROWS = 16
LAYERS = 2
CHIPS = 4
K = 4
KA = 4
LAG = 2
END = 3
D = 2
PF = 3
RING = 4
FR = 3
MOVE = 8
PRE = 4
PS = 8
PG = 3
G = 6
SLOTS = 24


def adamw(w, m, v, g):
    m = 0.9 * m + 0.1 * g
    v = 0.95 * v + 0.05 * g * g
    step = m * lax.rsqrt(v + 1e-8) + 0.1 * w
    return (w - 0.02 * step).astype(jnp.bfloat16), m, v


def kernel(geo, *refs):
    C, CD, NR, NC, CB = geo
    R = C // CD
    E = 4 * NC
    g, w, m, v = refs[0:3], refs[3:6], refs[6:9], refs[9:12]
    W, M, V, PT = refs[12:15], refs[15:18], refs[18:21], refs[21:24]
    (land, own, par, out, mb, vb, wb, wn, recv, credits, send, gsend, ownsem, parsem, d2d_recv, d2d_send, ld_sem, ww_sem,
     ag_recv, ag_send) = refs[24:]
    rep = lax.axis_index("rep")
    me = lax.axis_index("dp")
    z, c = me // 2, me % 2
    partner = (rep, z * 2 + 1 - c)
    nexts = ((rep, jnp.minimum(z + 1, CHIPS - 1) * 2 + c), (rep, jnp.maximum(z - 1, 0) * 2 + c))
    qs = (z, CHIPS - 1 - z)

    def split(j):
        mat = j // NR
        return mat // LAYERS, mat % LAYERS, j % NR

    def by_weight(j, body):
        k, l, r = split(j)
        for i in range(3):
            @pl.when(k == i)
            def _(i=i):
                body(i, l, r)

    def rows(i, dev, r):
        n = ROWS if i < 2 else ROWS * R
        return pl.ds(pl.multiple_of((dev * NR + r) * n, n), n)

    def load(i, src, dst, sem):
        if i < 2:
            pltpu.make_async_copy(src, dst, sem).start()
        else:
            for s in range(R):
                pltpu.make_async_copy(src.at[pl.ds(s * ROWS, ROWS), :], dst.at[:, pl.ds(s * CD, CD)], sem).start()

    def save(i, src, dst, sem):
        if i < 2:
            pltpu.make_async_copy(src, dst, sem).start()
        else:
            for s in range(R):
                pltpu.make_async_copy(src.at[:, pl.ds(s * CD, CD)], dst.at[pl.ds(s * ROWS, ROWS), :], sem).start()

    def wait_local(buf, sem):
        pltpu.make_async_copy(buf, buf, sem).wait()

    def decode(e):
        p = e - NC
        x = p - D
        first, last, head, tail = p < 0, p >= 2 * NC, p < D, p >= 2 * NC - D
        beta = jnp.where(first, 3, jnp.where(last, 0, jnp.where(head, 2, jnp.where(tail, 1, 1 + x % 2))))
        mid = jnp.where(x % 2 == 0, x // 2, D + x // 2)
        j = jnp.where(first, e, jnp.where(last, p - 2 * NC, jnp.where(head, p, jnp.where(tail, p - NC, mid))))
        return beta, j

    def sums(e, q):
        beta, j = decode(e)
        return (e >= 0) & (e < E) & ((q < beta) | ((q == beta) & (beta % 2 == 1))), beta, j

    def pair_index(b, i):
        n = NC // PG
        return jnp.where((b == 0) | (b == 3), 2 * i + jnp.where(b == 0, 1, 0), 2 * n + 2 * i + jnp.where(b == 1, 1, 0))

    def pair_group(i):
        n = NC // PG
        late = i >= 2 * n
        odd = i % 2
        b = jnp.where(late, 2 - odd, 3 - 3 * odd)
        return b, jnp.where(late, i - 2 * n, i) // 2

    def pair_wait(sem):
        many = land.at[0, pl.ds(0, PG)]
        pltpu.make_async_copy(many, many, sem).wait()

    def pair_push(i):
        @pl.when(i < 4 * NC // PG)
        def _():
            @pl.when(i >= PS)
            def _():
                pair_wait(d2d_send.at[i % PS])
            b, group = pair_group(i)

            def go(k, l, r):
                n = (ROWS if k < 2 else ROWS * R) * PG
                src = pl.ds(pl.multiple_of(((2 * b + 1 - c) * NR + r) * (n // PG), n), n)
                dst = pl.ds(pl.multiple_of(r * (n // PG), n), n)
                pltpu.make_async_remote_copy(
                    g[k].at[0, l, src, :], PT[k].at[l, b, dst, :], d2d_send.at[i % PS], d2d_recv.at[i],
                    device_id=partner, device_id_type=MESH).start()

            by_weight(group * PG, go)

    def prefetch(d, e):
        need, beta, j = sums(e, qs[d])
        b = beta if d == 0 else CHIPS - 1 - beta

        @pl.when(need)
        def _():
            s = e % RING
            by_weight(j, lambda k, l, r: load(k, g[k].at[0, l, rows(k, 2 * b + c, r), :], own.at[d, s], ownsem.at[d, s]))

            @pl.when(j % PG == 0)
            def _():
                pair_wait(d2d_recv.at[pair_index(b, j // PG)])

            by_weight(j, lambda k, l, r: load(k, PT[k].at[l, b, rows(k, 0, r), :], par.at[d, s], parsem.at[d, s]))

    def step_load(j):
        @pl.when(j < NC)
        def _():
            s = j % FR

            def go(k, l, r):
                load(k, m[k].at[l, rows(k, 0, r), :], mb.at[s], ld_sem.at[0, s])
                load(k, v[k].at[l, rows(k, 0, r), :], vb.at[s], ld_sem.at[1, s])
                load(k, w[k].at[l, rows(k, me, r), :], wb.at[s], ld_sem.at[2, s])

            by_weight(j, go)

    def wait_sum(d, n):
        pltpu.make_async_copy(out.at[d, 0], out.at[d, 0], send.at[d, n % K]).wait()

    def wait_gather(d, n):
        pltpu.make_async_copy(out.at[d, 0], out.at[d, 0], gsend.at[d, n % KA]).wait()

    def wait_recv(d, n):
        pltpu.make_async_copy(land.at[d, 0], land.at[d, 0], recv.at[d, n % SLOTS]).wait()

    def credit(d, n):
        @pl.when((n >= SLOTS) & (n % G == 0))
        def _():
            pl.semaphore_wait(credits.at[d], 1)

    def columns(body):
        def step(i, _):
            body(pl.ds(pl.multiple_of(i * CB, CB), CB))
            return 0

        lax.fori_loop(0, C // CB, step, 0)

    def weight(k, l, dev, r):
        return W[k].at[l, rows(k, dev, r), :]

    def gather_send(d, j, dev, i, n):
        @pl.when(i >= KA)
        def _():
            wait_gather(d, i)

        credit(d, n)

        def go(k, l, r):
            pltpu.make_async_remote_copy(
                weight(k, l, dev, r), weight(k, l, dev, r), gsend.at[d, i % KA], recv.at[d, n % SLOTS],
                device_id=nexts[d], device_id_type=MESH).start()

        by_weight(j, go)

    def partner_push(j, dev):
        def go(k, l, r):
            mat = k * LAYERS + l
            pltpu.make_async_remote_copy(
                weight(k, l, dev, r), weight(k, l, dev, r), ag_send.at[mat], ag_recv.at[mat],
                device_id=partner, device_id_type=MESH).start()

        by_weight(j, go)

    def handle(d, t):
        q = qs[d]
        e = t - LAG * q - jnp.where(q == CHIPS - 1, END, 0)
        valid = (e >= 0) & (e < E)
        beta, j = decode(e)
        b = beta if d == 0 else CHIPS - 1 - beta
        dev = 2 * b + c
        s = e % RING

        @pl.when(valid & (q < beta))
        def _():
            wait_local(own.at[d, s], ownsem.at[d, s])
            wait_local(par.at[d, s], parsem.at[d, s])
            i = jnp.where((q == 1) & (beta == 2), NC + j, e)
            o = i % K

            @pl.when(i >= K)
            def _():
                wait_sum(d, i)

            credit(d, e)

            @pl.when(q == 0)
            def _():
                def body(col):
                    total = own[d, s, :, col].astype(jnp.float32) + par[d, s, :, col].astype(jnp.float32)
                    out[d, o, :, col] = total.astype(jnp.bfloat16)

                columns(body)

            @pl.when(q > 0)
            def _():
                wait_recv(d, e)

                def body(col):
                    total = own[d, s, :, col].astype(jnp.float32) + par[d, s, :, col].astype(jnp.float32)
                    out[d, o, :, col] = (total + land[d, e % SLOTS, :, col].astype(jnp.float32)).astype(jnp.bfloat16)

                columns(body)

            pltpu.make_async_remote_copy(
                out.at[d, o], land.at[d, e % SLOTS], send.at[d, o], recv.at[d, e % SLOTS],
                device_id=nexts[d], device_id_type=MESH).start()

        @pl.when(valid & (q == beta) & (beta % 2 == 1))
        def _():
            f = j % FR
            wait_local(own.at[d, s], ownsem.at[d, s])
            wait_local(par.at[d, s], parsem.at[d, s])
            wait_local(mb.at[f], ld_sem.at[0, f])
            wait_local(vb.at[f], ld_sem.at[1, f])
            wait_local(wb.at[f], ld_sem.at[2, f])
            wait_recv(d, e)
            other = NC + jnp.where(j < D, j, 2 * j - D + 1)

            def update(extra, k, l, r):
                for p in range(1 if k < 2 else R):
                    rr = pl.ds(pl.multiple_of((r if k < 2 else r * R + p) * ROWS, ROWS), ROWS)
                    width = C if k < 2 else CD

                    def body(i, _, p=p, rr=rr, width=width):
                        col = pl.ds(pl.multiple_of(p * width + i * CB, CB), CB)
                        to = pl.ds(pl.multiple_of(i * CB, CB), CB)
                        total = own[d, s, :, col].astype(jnp.float32) + par[d, s, :, col].astype(jnp.float32)
                        total = total + land[d, e % SLOTS, :, col].astype(jnp.float32)
                        if extra:
                            total = total + land[1 - d, other % SLOTS, :, col].astype(jnp.float32)
                        grad = total.astype(jnp.bfloat16).astype(jnp.float32)
                        wn[f, :, col], M[k][l, rr, to], V[k][l, rr, to] = adamw(
                            wb[f, :, col].astype(jnp.float32), mb[f, :, col], vb[f, :, col], grad)
                        return 0

                    lax.fori_loop(0, width // CB, body, 0)

            @pl.when(beta == 1)
            def _():
                wait_recv(1 - d, other)
                by_weight(j, functools.partial(update, True))

            @pl.when(beta == 3)
            def _():
                by_weight(j, functools.partial(update, False))

            by_weight(j, lambda k, l, r: save(k, wn.at[f], weight(k, l, me, r), ww_sem))
            wait_local(wn.at[f], ww_sem)

            @pl.when(beta == 1)
            def _():
                gather_send(d, j, dev, j, e)
                gather_send(1 - d, j, dev, 2 * j, NC + 2 * j)

            partner_push(j, dev)
            step_load(j + FR - 1)

        @pl.when(valid & (q == beta) & (beta == 0))
        def _():
            gather_send(d, j, dev, j, e)

        @pl.when(valid & (q == CHIPS - 1) & (beta == 1))
        def _():
            wait_recv(d, NC + 2 * j)
            partner_push(j, dev + jnp.where(d == 0, 2, -2))

        @pl.when(valid & (q > beta) & (beta != 2))
        def _():
            two = beta == 1
            wait_recv(d, jnp.where(two & (q == CHIPS - 1), NC + 2 * j + 1, e))

            @pl.when(q < CHIPS - 1)
            def _():
                i = jnp.where(q == 1, NC + j, jnp.where(two, 2 * j + 1, 2 * NC + j))
                gather_send(d, j, dev, i, jnp.where(two, NC + 2 * j + 1, e))

            partner_push(j, dev)

        done = e - 2 * D

        @pl.when(valid & (q > 0) & (done >= 0) & (done % G == G - 1) & (done < E - SLOTS))
        def _():
            pl.semaphore_signal(credits.at[d], inc=1, device_id=nexts[1 - d], device_id_type=MESH)

        prefetch(d, e + PF)

    barrier = pltpu.get_barrier_semaphore()
    pl.semaphore_signal(barrier, inc=1, device_id=partner, device_id_type=MESH)
    for d in range(2):
        @pl.when(qs[d] < CHIPS - 1)
        def _(d=d):
            pl.semaphore_signal(barrier, inc=1, device_id=nexts[d], device_id_type=MESH)
    for j in range(FR - 1):
        step_load(jnp.int32(j))
    inner = (z > 0) & (z < CHIPS - 1)
    pl.semaphore_wait(barrier, jnp.where(inner, 3, 2))

    def before(i, _):
        pair_push(i)
        return 0

    lax.fori_loop(0, PRE, before, 0)

    def slot(i, _):
        t = i - PF
        pair_push(i + PRE)
        handle(0, t)
        handle(1, t)
        return 0

    lax.fori_loop(0, PF + E + LAG * (CHIPS - 1) + END, slot, 0)

    for d in range(2):
        @pl.when(qs[d] < CHIPS - 1)
        def _(d=d):
            for s in range(K):
                wait_sum(d, s)
            for s in range(KA):
                wait_gather(d, s)
    for s in range(PS):
        pair_wait(d2d_send.at[s])
    for k in range(3):
        half = W[k].shape[1] // 2
        for l in range(LAYERS):
            for sem in (ag_send, ag_recv):
                pltpu.make_async_copy(
                    W[k].at[l, pl.ds(0, half), :], W[k].at[l, pl.ds(0, half), :], sem.at[k * LAYERS + l]).wait()


def place(cuts, *refs):
    src, dst = refs[:9], refs[9:18]
    big, small, held_sem, in_sem, out_sem = refs[18:]
    held = [pltpu.make_async_copy(src[3 + i], dst[3 + i], held_sem.at[i]) for i in range(6)]
    moves = []
    for k in range(3):
        n = src[k].shape[1] // cuts
        for l in range(LAYERS):
            for i in range(cuts):
                s = len(moves) % MOVE
                buf = (big if k < 2 else small).at[s]
                at = (l, pl.ds(i * n, n), slice(None))
                moves.append((pltpu.make_async_copy(src[k].at[at], buf, in_sem.at[s]),
                              pltpu.make_async_copy(buf, dst[k].at[at], out_sem.at[s])))
    ahead = MOVE // 2
    for i in range(len(moves) + ahead):
        if i < len(moves):
            if i >= MOVE:
                moves[i - MOVE][1].wait()
            moves[i][0].start()
        if i == ahead:
            for copy in held:
                copy.start()
        if i >= ahead:
            moves[i - ahead][0].wait()
            moves[i - ahead][1].start()
    for _, out in moves[-MOVE:]:
        out.wait()
    for copy in held:
        copy.wait()


def step(*arrays):
    g, w, m, v = (arrays[i : i + 3] for i in (0, 3, 6, 9))
    C, CD = w[0].shape[2], w[2].shape[2]
    NR = m[0].shape[1] // ROWS
    NC = NR * LAYERS * 3
    CB = 384 if CD % 384 == 0 else CD
    geo = (C, CD, NR, NC, CB)
    E = 4 * NC
    bf, f32 = jnp.bfloat16, jnp.float32
    hbm, vmem = pl.BlockSpec(memory_space=pl.ANY), pl.BlockSpec(memory_space=pltpu.VMEM)
    outs = [jax.ShapeDtypeStruct(x.shape, x.dtype) for x in w]
    outs += [pltpu.VMEM(x.shape, x.dtype) for x in (*m, *v)]
    outs += [jax.ShapeDtypeStruct((LAYERS, CHIPS, *x.shape[1:]), bf) for x in m]
    dma = pltpu.SemaphoreType.DMA
    got = pl.pallas_call(
        functools.partial(kernel, geo),
        out_shape=outs,
        in_specs=[hbm] * 12,
        out_specs=[hbm] * 3 + [vmem] * 6 + [hbm] * 3,
        scratch_shapes=[
            pltpu.VMEM((2, SLOTS, ROWS, C), bf),
            pltpu.VMEM((2, RING, ROWS, C), bf),
            pltpu.VMEM((2, RING, ROWS, C), bf),
            pltpu.VMEM((2, K, ROWS, C), bf),
            pltpu.VMEM((FR, ROWS, C), f32),
            pltpu.VMEM((FR, ROWS, C), f32),
            pltpu.VMEM((FR, ROWS, C), bf),
            pltpu.VMEM((FR, ROWS, C), bf),
            dma((2, SLOTS)),
            pltpu.SemaphoreType.REGULAR((2,)),
            dma((2, K)),
            dma((2, KA)),
            dma((2, RING)),
            dma((2, RING)),
            dma((E // PG,)),
            dma((PS,)),
            dma((3, FR)),
            dma(()),
            dma((3 * LAYERS,)),
            dma((3 * LAYERS,)),
        ],
        compiler_params=pltpu.CompilerParams(collective_id=0, has_side_effects=True, vmem_limit_bytes=20 << 20),
        name="step",
    )(*arrays)
    held = [pltpu.with_memory_space_constraint(x, pltpu.VMEM) for x in got[3:9]]
    big, small = (w[0].shape[1] // 12, C), (w[2].shape[1] // 12, CD)
    return pl.pallas_call(
        functools.partial(place, 12),
        out_shape=[jax.ShapeDtypeStruct(x.shape, x.dtype) for x in (*w, *m, *v)],
        in_specs=[hbm] * 3 + [vmem] * 6,
        out_specs=[hbm] * 9,
        scratch_shapes=[
            pltpu.VMEM((MOVE, *big), bf),
            pltpu.VMEM((MOVE, *small), bf),
            dma((6,)),
            dma((MOVE,)),
            dma((MOVE,)),
        ],
        compiler_params=pltpu.CompilerParams(vmem_limit_bytes=20 << 20),
        name="place",
    )(*got[:3], *held)


def solution(mesh):
    all_of, cut = P(None, None, None), P(None, "dp", None)
    return jax.shard_map(
        step,
        mesh=mesh,
        in_specs=(P(("rep", "dp"), None, None, None),) * 3 + (all_of,) * 3 + (cut,) * 6,
        out_specs=(P("rep", None, None),) * 3 + (P("rep", "dp", None),) * 6,
        check_vma=False,
    )
```

profile of v0, /device:TPU:0, one launch (start us, length us, event | category | flops | bytes accessed | tf_op | source)
XLA Modules:
  0.0 762.7 jit_solution(538217251844508785)
XLA Ops:
  0.6 708.8 %step.1 = (bf16[2,1152,4608]{2,1,0:T(8,128)(2,1)}, bf16[2,1152,4608]{2,1,0:T(8,128)(2,1)}, bf16[2,4608,1152]{2,1,0:T(8,128)(2,1)}, f32[2,144,4608]{2,1,0:T(8,128...) custom-call(bf16[1,2,1152,4608]{3,2,1,0:T(8,128)(2,1)} %refs_0_.1, ...), custom_call_target="tpu_custom_call" | custom-call | tf_op jit(solution)/shard_map/step/pallas_call | solution.py:416
  709.4 53.3 %place.1 = (bf16[2,1152,4608]{2,1,0:T(8,128)(2,1)}, bf16[2,1152,4608]{2,1,0:T(8,128)(2,1)}, bf16[2,4608,1152]{2,1,0:T(8,128)(2,1)}, f32[2,144,4608]{2,1,0:T(8,12...) custom-call(bf16[2,1152,4608]{2,1,0:T(8,128)(2,1)} %get-tuple-elemen, ...), custom_call_target="tpu_custom_call" | custom-call | tf_op jit(solution)/shard_map/place/pallas_call | solution.py:448
where the time goes:
time: 763 us
  Pallas kernels  762 us (100%)
    pallas_call x1, Pallas kernels, step(): pl.pallas_call(functools.partial(kernel, geo), out_shape=outs, in_specs=[...  709 us
    pallas_call x1, Pallas kernels, step(): pl.pallas_call(functools.partial(place, 12), out_shape=[jax.ShapeDtypeStr...  53.3 us

commit v1 on v0

--- a/solution.py
+++ b/solution.py
@@ -6,6 +6,7 @@
 from jax.experimental import pallas as pl
 from jax.experimental.pallas import tpu as pltpu
 from jax.sharding import PartitionSpec as P
+
 
 MESH = pl.DeviceIdType.MESH
 ROWS = 16
@@ -16,15 +17,19 @@
 LAG = 2
 END = 3
 D = 2
-PF = 3
-RING = 4
-FR = 3
+PF = 2
+RING = 3
+FR = 2
+CUTS = 12
 MOVE = 8
+U = 4
+VMEM_LIMIT = 10 << 20
+HELD = 1
 PRE = 4
 PS = 8
 PG = 3
 G = 6
-SLOTS = 24
+SLOTS = 18
 
 
 def adamw(w, m, v, g):
@@ -39,9 +44,9 @@
     R = C // CD
     E = 4 * NC
     g, w, m, v = refs[0:3], refs[3:6], refs[6:9], refs[9:12]
-    W, M, V, PT = refs[12:15], refs[15:18], refs[18:21], refs[21:24]
+    W, M, V, seed, PT = refs[12:15], refs[15:18], refs[18:21], refs[21], refs[22:25]
     (land, own, par, out, mb, vb, wb, wn, recv, credits, send, gsend, ownsem, parsem, d2d_recv, d2d_send, ld_sem, ww_sem,
-     ag_recv, ag_send) = refs[24:]
+     ag_recv, ag_send) = refs[25:]
     rep = lax.axis_index("rep")
     me = lax.axis_index("dp")
     z, c = me // 2, me % 2
@@ -115,6 +120,7 @@
             @pl.when(i >= PS)
             def _():
                 pair_wait(d2d_send.at[i % PS])
+
             b, group = pair_group(i)
 
             def go(k, l, r):
@@ -204,7 +210,9 @@
     def handle(d, t):
         q = qs[d]
         e = t - LAG * q - jnp.where(q == CHIPS - 1, END, 0)
-        valid = (e >= 0) & (e < E)
+        sent = NC - (q + 1) * U
+        came = jnp.where(q == 0, sent, sent + U)
+        valid = (e >= 0) & (e < 3 * NC + came)
         beta, j = decode(e)
         b = beta if d == 0 else CHIPS - 1 - beta
         dev = 2 * b + c
@@ -269,8 +277,12 @@
                         if extra:
                             total = total + land[1 - d, other % SLOTS, :, col].astype(jnp.float32)
                         grad = total.astype(jnp.bfloat16).astype(jnp.float32)
-                        wn[f, :, col], M[k][l, rr, to], V[k][l, rr, to] = adamw(
+                        new, M[k][l, rr, to], V[k][l, rr, to] = adamw(
                             wb[f, :, col].astype(jnp.float32), mb[f, :, col], vb[f, :, col], grad)
+                        if k < HELD:
+                            W[k][l, rows(k, me, r), to] = new
+                        else:
+                            wn[f, :, col] = new
                         return 0
 
                     lax.fori_loop(0, width // CB, body, 0)
@@ -284,8 +296,12 @@
             def _():
                 by_weight(j, functools.partial(update, False))
 
-            by_weight(j, lambda k, l, r: save(k, wn.at[f], weight(k, l, me, r), ww_sem))
-            wait_local(wn.at[f], ww_sem)
+            def put(k, l, r):
+                if k >= HELD:
+                    save(k, wn.at[f], weight(k, l, me, r), ww_sem)
+                    wait_local(wn.at[f], ww_sem)
+
+            by_weight(j, put)
 
             @pl.when(beta == 1)
             def _():
@@ -309,7 +325,7 @@
             two = beta == 1
             wait_recv(d, jnp.where(two & (q == CHIPS - 1), NC + 2 * j + 1, e))
 
-            @pl.when(q < CHIPS - 1)
+            @pl.when((q < CHIPS - 1) & ((beta > 0) | (j < sent)))
             def _():
                 i = jnp.where(q == 1, NC + j, jnp.where(two, 2 * j + 1, 2 * NC + j))
                 gather_send(d, j, dev, i, jnp.where(two, NC + 2 * j + 1, e))
@@ -318,7 +334,7 @@
 
         done = e - 2 * D
 
-        @pl.when(valid & (q > 0) & (done >= 0) & (done % G == G - 1) & (done < E - SLOTS))
+        @pl.when(valid & (q > 0) & (done >= 0) & (done % G == G - 1) & (done + 1 - G + SLOTS < 3 * NC + came))
         def _():
             pl.semaphore_signal(credits.at[d], inc=1, device_id=nexts[1 - d], device_id_type=MESH)
 
@@ -359,48 +375,106 @@
                 wait_gather(d, s)
     for s in range(PS):
         pair_wait(d2d_send.at[s])
-    for k in range(3):
-        half = W[k].shape[1] // 2
+
+    def pushed(k, l, chunks):
+        if chunks:
+            n = chunks * (ROWS if k < 2 else ROWS * R)
+            for sem in (ag_send, ag_recv):
+                pltpu.make_async_copy(W[k].at[l, pl.ds(0, n), :], W[k].at[l, pl.ds(0, n), :], sem.at[k * LAYERS + l]).wait()
+
+    for k in range(2):
         for l in range(LAYERS):
-            for sem in (ag_send, ag_recv):
-                pltpu.make_async_copy(
-                    W[k].at[l, pl.ds(0, half), :], W[k].at[l, pl.ds(0, half), :], sem.at[k * LAYERS + l]).wait()
-
-
-def place(cuts, *refs):
-    src, dst = refs[:9], refs[9:18]
-    big, small, held_sem, in_sem, out_sem = refs[18:]
-    held = [pltpu.make_async_copy(src[3 + i], dst[3 + i], held_sem.at[i]) for i in range(6)]
+            pushed(k, l, CHIPS * NR)
+    for at in range(CHIPS):
+        @pl.when(z == at)
+        def _(at=at):
+            for l in range(LAYERS):
+                start = (2 * LAYERS + l) * NR
+                here = [NC - far * U for far in (at, CHIPS - 1 - at)]
+                pushed(2, l, 2 * NR + sum(min(max(n - start, 0), NR) for n in here))
+
+    for d in range(2):
+        @pl.when((c == d) & (qs[d] < CHIPS - 1))
+        def _(d=d):
+            for lane in range(2):
+                for i in range(U):
+                    _, l, r = split(NC - (qs[d] + 1) * U + i)
+                    block = (0 if d == 0 else CHIPS - 1) * 2 + lane
+                    pltpu.make_async_copy(weight(2, l, block, r), seed.at[lane * U + i], ww_sem).start()
+            wait_local(seed, ww_sem)
+
+
+def place_held(*refs):
+    n = len(refs) // 2
+    for i in range(n):
+        parts = 4 if i < HELD else 1
+        rows = refs[i].shape[1] // parts
+        for l in range(LAYERS):
+            for p in range(parts):
+                at = (l, pl.ds(p * rows, rows), slice(None))
+                pltpu.make_async_copy(refs[i].at[at], refs[n + i].at[at], refs[-1].at[i]).start()
+    for i in range(n):
+        pltpu.make_async_copy(refs[i], refs[n + i], refs[-1].at[i]).wait()
+
+
+def place(cuts, src, dst, ring, in_sem, out_sem):
+    n = src.shape[1] // cuts
     moves = []
-    for k in range(3):
-        n = src[k].shape[1] // cuts
-        for l in range(LAYERS):
-            for i in range(cuts):
-                s = len(moves) % MOVE
-                buf = (big if k < 2 else small).at[s]
-                at = (l, pl.ds(i * n, n), slice(None))
-                moves.append((pltpu.make_async_copy(src[k].at[at], buf, in_sem.at[s]),
-                              pltpu.make_async_copy(buf, dst[k].at[at], out_sem.at[s])))
+    for l in range(LAYERS):
+        for i in range(cuts):
+            at, s = (l, pl.ds(i * n, n), slice(None)), len(moves) % MOVE
+            moves.append((pltpu.make_async_copy(src.at[at], ring.at[s], in_sem.at[s]),
+                          pltpu.make_async_copy(ring.at[s], dst.at[at], out_sem.at[s])))
     ahead = MOVE // 2
     for i in range(len(moves) + ahead):
         if i < len(moves):
             if i >= MOVE:
                 moves[i - MOVE][1].wait()
             moves[i][0].start()
-        if i == ahead:
-            for copy in held:
-                copy.start()
         if i >= ahead:
             moves[i - ahead][0].wait()
             moves[i - ahead][1].start()
     for _, out in moves[-MOVE:]:
         out.wait()
-    for copy in held:
-        copy.wait()
+
+
+def fill(geo, rounds, old, *refs):
+    C, CD, NR, NC, _ = geo
+    R = C // CD
+    n = len(rounds)
+    got, swapped, new, sem = refs[:n], refs[n : 2 * n], refs[2 * n], refs[2 * n + 1]
+    me = lax.axis_index("dp")
+    z, c = me // 2, me % 2
+    qs = (z, CHIPS - 1 - z)
+    h = ROWS * R
+
+    def each(body):
+        for a, r in enumerate(rounds):
+            for d in range(2):
+                @pl.when(qs[d] >= r)
+                def _(a=a, r=r, d=d):
+                    body(a, r, d, sem.at[a * 2 + d])
+
+    def put(a, r, d, sem):
+        for lane in range(2):
+            for i in range(U):
+                j = NC - qs[d] * U + (r - 1) * U + i - 2 * LAYERS * NR
+                block = (0 if d == 0 else CHIPS - 1) * 2 + lane
+                to = new.at[j // NR, pl.ds(pl.multiple_of((block * NR + j % NR) * h, h), h), :]
+                for mine, src in ((True, got[a]), (False, swapped[a])):
+                    @pl.when((c == d) == mine)
+                    def _(src=src, to=to, lane=lane, i=i):
+                        pltpu.make_async_copy(src.at[lane * U + i], to, sem).start()
+
+    def end(a, r, d, sem):
+        pltpu.make_async_copy(got[a], got[a], sem).wait()
+
+    each(put)
+    each(end)
 
 
 def step(*arrays):
-    g, w, m, v = (arrays[i : i + 3] for i in (0, 3, 6, 9))
+    _, w, m, v = (arrays[i : i + 3] for i in (0, 3, 6, 9))
     C, CD = w[0].shape[2], w[2].shape[2]
     NR = m[0].shape[1] // ROWS
     NC = NR * LAYERS * 3
@@ -409,15 +483,17 @@
     E = 4 * NC
     bf, f32 = jnp.bfloat16, jnp.float32
     hbm, vmem = pl.BlockSpec(memory_space=pl.ANY), pl.BlockSpec(memory_space=pltpu.VMEM)
-    outs = [jax.ShapeDtypeStruct(x.shape, x.dtype) for x in w]
+    outs = [pltpu.VMEM(x.shape, x.dtype) for x in w[:HELD]] + [jax.ShapeDtypeStruct(x.shape, x.dtype) for x in w[HELD:]]
     outs += [pltpu.VMEM(x.shape, x.dtype) for x in (*m, *v)]
+    piece = (2 * U, ROWS * (C // CD), CD)
+    outs += [pltpu.VMEM(piece, bf)]
     outs += [jax.ShapeDtypeStruct((LAYERS, CHIPS, *x.shape[1:]), bf) for x in m]
     dma = pltpu.SemaphoreType.DMA
     got = pl.pallas_call(
         functools.partial(kernel, geo),
         out_shape=outs,
         in_specs=[hbm] * 12,
-        out_specs=[hbm] * 3 + [vmem] * 6 + [hbm] * 3,
+        out_specs=[vmem] * HELD + [hbm] * (3 - HELD) + [vmem] * 7 + [hbm] * 3,
         scratch_shapes=[
             pltpu.VMEM((2, SLOTS, ROWS, C), bf),
             pltpu.VMEM((2, RING, ROWS, C), bf),
@@ -440,30 +516,74 @@
             dma((3 * LAYERS,)),
             dma((3 * LAYERS,)),
         ],
-        compiler_params=pltpu.CompilerParams(collective_id=0, has_side_effects=True, vmem_limit_bytes=20 << 20),
+        compiler_params=pltpu.CompilerParams(collective_id=0, has_side_effects=True, vmem_limit_bytes=VMEM_LIMIT),
         name="step",
     )(*arrays)
-    held = [pltpu.with_memory_space_constraint(x, pltpu.VMEM) for x in got[3:9]]
-    big, small = (w[0].shape[1] // 12, C), (w[2].shape[1] // 12, CD)
-    return pl.pallas_call(
-        functools.partial(place, 12),
-        out_shape=[jax.ShapeDtypeStruct(x.shape, x.dtype) for x in (*w, *m, *v)],
-        in_specs=[hbm] * 3 + [vmem] * 6,
-        out_specs=[hbm] * 9,
-        scratch_shapes=[
-            pltpu.VMEM((MOVE, *big), bf),
-            pltpu.VMEM((MOVE, *small), bf),
-            dma((6,)),
-            dma((MOVE,)),
-            dma((MOVE,)),
-        ],
-        compiler_params=pltpu.CompilerParams(vmem_limit_bytes=20 << 20),
-        name="place",
-    )(*got[:3], *held)
+    seed = got[9]
+    in_vmem = [pltpu.with_memory_space_constraint(got[i], pltpu.VMEM) for i in (*range(HELD), *range(3, 9))]
+    local = pltpu.CompilerParams(vmem_limit_bytes=VMEM_LIMIT)
+
+    def onward(first):
+        there = [(2 * p, 2 * p + 2) for p in range(first, CHIPS - 1)]
+        return there + [(2 * CHIPS - 1 - a, 2 * CHIPS - 1 - b) for a, b in there]
+
+    got_by, swapped = [], []
+    for r in range(CHIPS - 1):
+        seed = lax.ppermute(seed, "dp", onward(r))
+        got_by.append(pltpu.with_memory_space_constraint(seed, pltpu.VMEM))
+        other = lax.ppermute(seed, "dp", [(i, i ^ 1) for i in range(2 * CHIPS)])
+        swapped.append(pltpu.with_memory_space_constraint(other, pltpu.VMEM))
+
+    def cost(n):
+        return pl.CostEstimate(flops=n, bytes_accessed=n, transcendentals=0)
+
+    def move(k):
+        shape = w[k].shape
+        return pl.pallas_call(
+            functools.partial(place, CUTS),
+            out_shape=jax.ShapeDtypeStruct(shape, bf),
+            in_specs=[hbm],
+            out_specs=hbm,
+            scratch_shapes=[pltpu.VMEM((MOVE, shape[1] // CUTS, shape[2]), bf), dma((MOVE,)), dma((MOVE,))],
+            compiler_params=local,
+            cost_estimate=cost(4 * w[k].size),
+        )(pltpu.with_memory_space_constraint(got[k], pltpu.HBM))
+
+    def take(rounds, old):
+        n = len(rounds)
+        return pl.pallas_call(
+            functools.partial(fill, geo, rounds),
+            out_shape=jax.ShapeDtypeStruct(old.shape, bf),
+            in_specs=[hbm] + [vmem] * (2 * n),
+            out_specs=hbm,
+            scratch_shapes=[dma((2 * n,))],
+            input_output_aliases={0: 0},
+            compiler_params=local,
+            cost_estimate=cost(4 * n * 6 * U * 1000),
+        )(old, *(got_by[r - 1] for r in rounds), *(swapped[r - 1] for r in rounds))
+
+    shapes = [x.shape for x in w[:HELD]] + [x.shape for x in (*m, *v)]
+    types = [bf] * HELD + [f32] * 6
+    placed = pl.pallas_call(
+        place_held,
+        out_shape=[jax.ShapeDtypeStruct(a, b) for a, b in zip(shapes, types, strict=True)],
+        in_specs=[vmem] * len(in_vmem),
+        out_specs=[hbm] * len(in_vmem),
+        scratch_shapes=[dma((len(in_vmem),))],
+        compiler_params=local,
+        cost_estimate=cost(8 * w[0].size),
+        name="place_held",
+    )(*in_vmem)
+    up = move(1)
+    down = move(2)
+    down = take((1, 2), down)
+    down = take((3,), down)
+    return (placed[0], up, down, *placed[1:])
 
 
 def solution(mesh):
     all_of, cut = P(None, None, None), P(None, "dp", None)
+
     return jax.shard_map(
         step,
         mesh=mesh,

time: 763 us -> 788 us (1.033)
  starting transfers between devices: 0 us -> 40.9 us
  Pallas kernels: 762 us -> 732 us
  waiting for transfers between devices: 0 us -> 13.6 us
    ppermute x0 -> x6, starting transfers between devices: none -> 40.9 us  [the longest x3 32.7 us: step(): other = lax.ppermute(seed, 'dp', [(i, i ^ 1) for i in range(2 * CHIPS)])]
    pallas_call x1, Pallas kernels: 709 us -> 679 us  [step(): pl.pallas_call(functools.partial(kernel, geo), out_shape=outs, in_specs=[...]
    ppermute x0 -> x6, waiting for transfers between devices: none -> 13.6 us  [the longest x3 13.6 us: step(): seed = lax.ppermute(seed, 'dp', onward(r))]
    pallas_call x1 -> x5, Pallas kernels: 53.3 us -> 52.8 us  [the longest x2 30.2 us: move(): pl.pallas_call(functools.partial(place, CUTS), out_shape=jax.ShapeDtypeSt...]
  transfers between devices with their start and end apart: 0 -> 6, of which waited for: 0 -> 1; matrix products, arithmetic and copies ran while one was open for 0% -> 0% of each run, Pallas kernels for 0% -> 6%
where the time goes in v1:
time: 788 us; the launch traced here: 787 us
  Pallas kernels  732 us (93%)
  starting transfers between devices  40.9 us (5%)
  waiting for transfers between devices  13.6 us (2%)
    pallas_call x1, Pallas kernels, step(): pl.pallas_call(functools.partial(kernel, geo), out_shape=outs, in_specs=[...  679 us
    ppermute x3, starting transfers between devices, step(): other = lax.ppermute(seed, 'dp', [(i, i ^ 1) for i in range(2 * CHIPS)])  32.7 us
    pallas_call x2, Pallas kernels, move(): pl.pallas_call(functools.partial(place, CUTS), out_shape=jax.ShapeDtypeSt...  30.2 us
    pallas_call x1, Pallas kernels, step(): pl.pallas_call(place_held, out_shape=[jax.ShapeDtypeStruct(a, b) for a, b...  16.9 us
  transfers between devices with their start and end apart: 6, of which 1 were waited for; matrix products, arithmetic and copies ran while one was open for 0% of the time, Pallas kernels for 6%

profile of v1, /device:TPU:0, one launch (start us, length us, event | category | flops | bytes accessed | tf_op | source)
XLA Modules:
  0.0 787.1 jit_solution(3639483335870977444)
XLA Ops:
  0.6 679.0 %step.1 = (bf16[2,1152,4608]{2,1,0:T(8,128)(2,1)S(1)}, bf16[2,1152,4608]{2,1,0:T(8,128)(2,1)}, bf16[2,4608,1152]{2,1,0:T(8,128)(2,1)}, f32[2,144,4608]{2,1,0:T(8...) custom-call(bf16[1,2,1152,4608]{3,2,1,0:T(8,128)(2,1)} %refs_0_.1, ...), custom_call_target="tpu_custom_call" | custom-call | tf_op jit(solution)/shard_map/step/pallas_call | solution.py:492
  679.7 5.7 collective-permute-start
  685.4 13.6 %collective-permute-done.refs_0_ = bf16[8,64,1152]{2,1,0:T(8,128)(2,1)S(1)} collective-permute-done((bf16[8,64,1152]{2,1,0:T(8,128)(2,1)S(1)}, bf16[8,64,1152]{2,1,0:T(8,128)(2,1)S(1)}, u32[]{:S(2)}, u32[]{:S(2)}) %collective-permute-start) | collective-permute-done | bytes 1179680 | tf_op jit(solution)/shard_map/ppermute | solution.py:532
  699.1 1.7 collective-permute-start.1
  700.8 0.0 collective-permute-done.1.refs_1_
  700.8 0.7 collective-permute-start.4
  701.5 16.9 %collective-permute-start.2 = (bf16[8,64,1152]{2,1,0:T(8,128)(2,1)S(1)}, bf16[8,64,1152]{2,1,0:T(8,128)(2,1)}, u32[]{:S(2)}, u32[]{:S(2)}) collective-permute-start(bf16[8,64,1152]{2,1,0:T(8,128)(2,1)S(1)} %collective-permute-done.refs_0_), channel_id=1, source_target_pairs={{0,1},{1,0},{2,3},{3,2},{4,5},{5,4},{6,7},{7,6},{8,9},{9,8},{10,11... | collective-permute-start | bytes 3538952 | tf_op jit(solution)/shard_map/ppermute | solution.py:534
  718.4 0.1 collective-permute-start.3
  718.5 0.0 collective-permute-done.4.refs_0_
  718.5 15.7 %collective-permute-start.5 = (bf16[8,64,1152]{2,1,0:T(8,128)(2,1)S(1)}, bf16[8,64,1152]{2,1,0:T(8,128)(2,1)}, u32[]{:S(2)}, u32[]{:S(2)}) collective-permute-start(bf16[8,64,1152]{2,1,0:T(8,128)(2,1)S(1)} %collective-permute-done.4.refs_0_), channel_id=1, source_target_pairs={{0,1},{1,0},{2,3},{3,2},{4,5},{5,4},{6,7},{7,6},{8,9},{9,8},{10,11... | collective-permute-start | bytes 3538952 | tf_op jit(solution)/shard_map/ppermute | solution.py:534
  734.2 15.1 %shard_map.188.old = bf16[2,4608,1152]{2,1,0:T(8,128)(2,1)} custom-call(bf16[2,4608,1152]{2,1,0:T(8,128)(2,1)} %get-tuple-element.35.src), custom_call_target="tpu_custom_call" | custom-call | flops 42467328 | bytes 42467328 | tf_op jit(solution)/shard_map/pallas_call | solution.py:542
  749.3 15.1 %shard_map.187 = bf16[2,1152,4608]{2,1,0:T(8,128)(2,1)} custom-call(bf16[2,1152,4608]{2,1,0:T(8,128)(2,1)} %get-tuple-element.34.src), custom_call_target="tpu_custom_call" | custom-call | flops 42467328 | bytes 42467328 | tf_op jit(solution)/shard_map/pallas_call | solution.py:542
  764.4 16.9 %place_held.1 = (bf16[2,1152,4608]{2,1,0:T(8,128)(2,1)}, f32[2,144,4608]{2,1,0:T(8,128)}, f32[2,144,4608]{2,1,0:T(8,128)}, f32[2,576,1152]{2,1,0:T(8,128)}, f32[...) custom-call(bf16[2,1152,4608]{2,1,0:T(8,128)(2,1)S(1)} %get-tuple-element.26.refs_0_, ...), custom_call_target="tpu_custom_call" | custom-call | flops 84934656 | bytes 84934656 | tf_op jit(solution)/shard_map/place_held/pallas_call | solution.py:567
  781.3 0.0 collective-permute-done.2.refs_2_
  781.3 0.0 collective-permute-done.3.refs_3_
  781.3 3.4 shard_map.189.old
  784.8 0.0 collective-permute-done.5.refs_1_
  784.8 2.3 shard_map.190
Async XLA Ops:
  679.7 19.4 %collective-permute-start = (bf16[8,64,1152]{2,1,0:T(8,128)(2,1)S(1)}, bf16[8,64,1152]{2,1,0:T(8,128)(2,1)S(1)}, u32[]{:S(2)}, u32[]{:S(2)}) collective-permute-start(bf16[8,64,1152]{2,1,0:T(8,128)(2,1)S(1)} %get-tuple-element.36), channel_id=1, source_target_pairs={{0,2},{2,4},{4,6},{7,5},{5,3},{3,1},{8,10},{10,12},{12,14},{15,13}... | collective-permute-start | bytes 3538952 | tf_op jit(solution)/shard_map/ppermute | solution.py:532
  699.1 1.7 collective-permute-start.1
  700.8 17.7 %collective-permute-start.4 = (bf16[8,64,1152]{2,1,0:T(8,128)(2,1)}, bf16[8,64,1152]{2,1,0:T(8,128)(2,1)S(1)}, u32[]{:S(2)}, u32[]{:S(2)}) collective-permute-start(bf16[8,64,1152]{2,1,0:T(8,128)(2,1)} %collective-permute-done.1.refs_1_), channel_id=1, source_target_pairs={{4,6},{3,1},{12,14},{11,9},{20,22},{19,17},{28,30},{27,25}} | collective-permute-start | bytes 3538952 | tf_op jit(solution)/shard_map/ppermute | solution.py:532
  701.5 79.8 %collective-permute-start.2 = (bf16[8,64,1152]{2,1,0:T(8,128)(2,1)S(1)}, bf16[8,64,1152]{2,1,0:T(8,128)(2,1)}, u32[]{:S(2)}, u32[]{:S(2)}) collective-permute-start(bf16[8,64,1152]{2,1,0:T(8,128)(2,1)S(1)} %collective-permute-done.refs_0_), channel_id=1, source_target_pairs={{0,1},{1,0},{2,3},{3,2},{4,5},{5,4},{6,7},{7,6},{8,9},{9,8},{10,11... | collective-permute-start | bytes 3538952 | tf_op jit(solution)/shard_map/ppermute | solution.py:534
  718.4 62.9 %collective-permute-start.3 = (bf16[8,64,1152]{2,1,0:T(8,128)(2,1)}, bf16[8,64,1152]{2,1,0:T(8,128)(2,1)}, u32[]{:S(2)}, u32[]{:S(2)}) collective-permute-start(bf16[8,64,1152]{2,1,0:T(8,128)(2,1)} %collective-permute-done.1.refs_1_), channel_id=1, source_target_pairs={{0,1},{1,0},{2,3},{3,2},{4,5},{5,4},{6,7},{7,6},{8,9},{9,8},{10,11... | collective-permute-start | bytes 3538952 | tf_op jit(solution)/shard_map/ppermute | solution.py:534
  718.5 66.3 %collective-permute-start.5 = (bf16[8,64,1152]{2,1,0:T(8,128)(2,1)S(1)}, bf16[8,64,1152]{2,1,0:T(8,128)(2,1)}, u32[]{:S(2)}, u32[]{:S(2)}) collective-permute-start(bf16[8,64,1152]{2,1,0:T(8,128)(2,1)S(1)} %collective-permute-done.4.refs_0_), channel_id=1, source_target_pairs={{0,1},{1,0},{2,3},{3,2},{4,5},{5,4},{6,7},{7,6},{8,9},{9,8},{10,11... | collective-permute-start | bytes 3538952 | tf_op jit(solution)/shard_map/ppermute | solution.py:534

commit v2 on v1

--- a/solution.py
+++ b/solution.py
@@ -20,14 +20,15 @@
 PF = 2
 RING = 3
 FR = 2
-CUTS = 12
+CUTS = 24
 MOVE = 8
 U = 4
+HOPS = CHIPS - 1
 VMEM_LIMIT = 10 << 20
 HELD = 1
 PRE = 4
 PS = 8
-PG = 3
+PG = 9
 G = 6
 SLOTS = 18
 
@@ -45,8 +46,8 @@
     E = 4 * NC
     g, w, m, v = refs[0:3], refs[3:6], refs[6:9], refs[9:12]
     W, M, V, seed, PT = refs[12:15], refs[15:18], refs[18:21], refs[21], refs[22:25]
-    (land, own, par, out, mb, vb, wb, wn, recv, credits, send, gsend, ownsem, parsem, d2d_recv, d2d_send, ld_sem, ww_sem,
-     ag_recv, ag_send) = refs[25:]
+    (land, own, par, out, mb, vb, wb, wn, recv, credits, send, gsend, ownsem, parsem, d2d_recv, d2d_send, d2d_first, ld_sem, ww_sem,
+     ag_recv, ag_send, seed_sem) = refs[25:]
     rep = lax.axis_index("rep")
     me = lax.axis_index("dp")
     z, c = me // 2, me % 2
@@ -133,6 +134,12 @@
 
             by_weight(group * PG, go)
 
+    def first_push(d, e):
+        b = (CHIPS - 1) * (1 - d)
+        pltpu.make_async_remote_copy(
+            g[0].at[0, 0, rows(0, 2 * b + 1 - c, e), :], par.at[d, e], d2d_first.at[d, e], parsem.at[d, e],
+            device_id=partner, device_id_type=MESH).start()
+
     def prefetch(d, e):
         need, beta, j = sums(e, qs[d])
         b = beta if d == 0 else CHIPS - 1 - beta
@@ -142,11 +149,13 @@
             s = e % RING
             by_weight(j, lambda k, l, r: load(k, g[k].at[0, l, rows(k, 2 * b + c, r), :], own.at[d, s], ownsem.at[d, s]))
 
-            @pl.when(j % PG == 0)
+            @pl.when((j % PG == 0) & (e >= RING) | (e == RING))
             def _():
                 pair_wait(d2d_recv.at[pair_index(b, j // PG)])
 
-            by_weight(j, lambda k, l, r: load(k, PT[k].at[l, b, rows(k, 0, r), :], par.at[d, s], parsem.at[d, s]))
+            @pl.when(e >= RING)
+            def _():
+                by_weight(j, lambda k, l, r: load(k, PT[k].at[l, b, rows(k, 0, r), :], par.at[d, s], parsem.at[d, s]))
 
     def step_load(j):
         @pl.when(j < NC)
@@ -332,6 +341,22 @@
 
             partner_push(j, dev)
 
+        i = jnp.where(q == 0, j, j - sent)
+
+        @pl.when(valid & (beta == 0) & (q < CHIPS - 1) & (i >= 0) & (i < U))
+        def _():
+            _, l, r = split(sent + i)
+            src, dst = weight(2, l, dev, r), seed.at[c * U + i]
+
+            @pl.when(c == d)
+            def _():
+                pltpu.make_async_copy(src, dst, seed_sem.at[0]).start()
+
+            @pl.when(c != d)
+            def _():
+                pltpu.make_async_remote_copy(
+                    src, dst, seed_sem.at[1], seed_sem.at[2], device_id=partner, device_id_type=MESH).start()
+
         done = e - 2 * D
 
         @pl.when(valid & (q > 0) & (done >= 0) & (done % G == G - 1) & (done + 1 - G + SLOTS < 3 * NC + came))
@@ -355,6 +380,9 @@
         pair_push(i)
         return 0
 
+    for e in range(RING):
+        for d in range(2):
+            first_push(d, e)
     lax.fori_loop(0, PRE, before, 0)
 
     def slot(i, _):
@@ -375,6 +403,9 @@
                 wait_gather(d, s)
     for s in range(PS):
         pair_wait(d2d_send.at[s])
+    for e in range(RING):
+        for d in range(2):
+            wait_local(par.at[d, e], d2d_first.at[d, e])
 
     def pushed(k, l, chunks):
         if chunks:
@@ -393,49 +424,57 @@
                 here = [NC - far * U for far in (at, CHIPS - 1 - at)]
                 pushed(2, l, 2 * NR + sum(min(max(n - start, 0), NR) for n in here))
 
+    lane = seed.at[pl.ds(0, U)]
     for d in range(2):
         @pl.when((c == d) & (qs[d] < CHIPS - 1))
-        def _(d=d):
-            for lane in range(2):
-                for i in range(U):
-                    _, l, r = split(NC - (qs[d] + 1) * U + i)
-                    block = (0 if d == 0 else CHIPS - 1) * 2 + lane
-                    pltpu.make_async_copy(weight(2, l, block, r), seed.at[lane * U + i], ww_sem).start()
-            wait_local(seed, ww_sem)
-
-
-def place_held(*refs):
-    n = len(refs) // 2
+        def _():
+            wait_local(lane, seed_sem.at[0])
+            wait_local(lane, seed_sem.at[2])
+
+        @pl.when((c != d) & (qs[d] < CHIPS - 1))
+        def _():
+            wait_local(lane, seed_sem.at[1])
+
+
+def place(still, moved, *refs):
+    n, k = still, len(moved)
+    fresh = sum(old is None for _, old in moved)
+    held, src = refs[:n], refs[n : n + k]
+    outs = refs[n + k + (k - fresh) :]
+    held_out, dst, (ring, held_sem, in_sem, out_sem) = outs[:n], outs[n : n + k], (outs[n + k : -3], *outs[-3:])
+    moves = []
+    for i, (pieces, _) in enumerate(moved):
+        for at, buf in pieces:
+            s = len(moves) % MOVE
+            moves.append((pltpu.make_async_copy(src[i].at[at], ring[buf].at[s], in_sem.at[s]),
+                          pltpu.make_async_copy(ring[buf].at[s], dst[i].at[at], out_sem.at[s])))
+    copies = []
     for i in range(n):
-        parts = 4 if i < HELD else 1
-        rows = refs[i].shape[1] // parts
+        parts = 4 if held[i].dtype == jnp.bfloat16 else 1
+        rows = held[i].shape[1] // parts
         for l in range(LAYERS):
             for p in range(parts):
                 at = (l, pl.ds(p * rows, rows), slice(None))
-                pltpu.make_async_copy(refs[i].at[at], refs[n + i].at[at], refs[-1].at[i]).start()
-    for i in range(n):
-        pltpu.make_async_copy(refs[i], refs[n + i], refs[-1].at[i]).wait()
-
-
-def place(cuts, src, dst, ring, in_sem, out_sem):
-    n = src.shape[1] // cuts
-    moves = []
-    for l in range(LAYERS):
-        for i in range(cuts):
-            at, s = (l, pl.ds(i * n, n), slice(None)), len(moves) % MOVE
-            moves.append((pltpu.make_async_copy(src.at[at], ring.at[s], in_sem.at[s]),
-                          pltpu.make_async_copy(ring.at[s], dst.at[at], out_sem.at[s])))
+                copies.append(pltpu.make_async_copy(held[i].at[at], held_out[i].at[at], held_sem.at[i]))
     ahead = MOVE // 2
-    for i in range(len(moves) + ahead):
+    if not moves:
+        for copy in copies:
+            copy.start()
+    for i in range(len(moves) + ahead if moves else 0):
         if i < len(moves):
             if i >= MOVE:
                 moves[i - MOVE][1].wait()
             moves[i][0].start()
+        if i == ahead - 1:
+            for copy in copies:
+                copy.start()
         if i >= ahead:
             moves[i - ahead][0].wait()
             moves[i - ahead][1].start()
     for _, out in moves[-MOVE:]:
         out.wait()
+    for i in range(n):
+        pltpu.make_async_copy(held[i], held_out[i], held_sem.at[i]).wait()
 
 
 def fill(geo, rounds, old, *refs):
@@ -511,16 +550,17 @@
             dma((2, RING)),
             dma((E // PG,)),
             dma((PS,)),
+            dma((2, RING)),
             dma((3, FR)),
             dma(()),
             dma((3 * LAYERS,)),
             dma((3 * LAYERS,)),
+            dma((3,)),
         ],
         compiler_params=pltpu.CompilerParams(collective_id=0, has_side_effects=True, vmem_limit_bytes=VMEM_LIMIT),
         name="step",
     )(*arrays)
     seed = got[9]
-    in_vmem = [pltpu.with_memory_space_constraint(got[i], pltpu.VMEM) for i in (*range(HELD), *range(3, 9))]
     local = pltpu.CompilerParams(vmem_limit_bytes=VMEM_LIMIT)
 
     def onward(first):
@@ -528,26 +568,43 @@
         return there + [(2 * CHIPS - 1 - a, 2 * CHIPS - 1 - b) for a, b in there]
 
     got_by, swapped = [], []
-    for r in range(CHIPS - 1):
-        seed = lax.ppermute(seed, "dp", onward(r))
-        got_by.append(pltpu.with_memory_space_constraint(seed, pltpu.VMEM))
+    for r in range(1, HOPS + 1):
+        seed = lax.ppermute(seed, "dp", onward(r - 1))
+        seed = pltpu.with_memory_space_constraint(seed, pltpu.VMEM)
+        got_by.append(seed)
         other = lax.ppermute(seed, "dp", [(i, i ^ 1) for i in range(2 * CHIPS)])
         swapped.append(pltpu.with_memory_space_constraint(other, pltpu.VMEM))
 
     def cost(n):
         return pl.CostEstimate(flops=n, bytes_accessed=n, transcendentals=0)
 
-    def move(k):
-        shape = w[k].shape
+    def pieces(k, first, last):
+        n = w[k].shape[1] // CUTS
+        return [((i // CUTS, pl.ds(i % CUTS * n, n), slice(None)), 0 if k < 2 else 1) for i in range(first, last)]
+
+    def move(still, moved):
+        types = [jax.ShapeDtypeStruct(x.shape, x.dtype) for x in still]
+        types += [jax.ShapeDtypeStruct(w[k].shape, bf) for k, _, _ in moved]
+        olds = [old for _, _, old in moved if old is not None]
+        begin = len(still) + len(moved)
+        where = [len(still) + i for i, (_, _, old) in enumerate(moved) if old is not None]
         return pl.pallas_call(
-            functools.partial(place, CUTS),
-            out_shape=jax.ShapeDtypeStruct(shape, bf),
-            in_specs=[hbm],
-            out_specs=hbm,
-            scratch_shapes=[pltpu.VMEM((MOVE, shape[1] // CUTS, shape[2]), bf), dma((MOVE,)), dma((MOVE,))],
+            functools.partial(place, len(still), [(p, old) for _, p, old in moved]),
+            out_shape=types,
+            in_specs=[vmem] * len(still) + [hbm] * (len(moved) + len(olds)),
+            out_specs=[hbm] * len(types),
+            scratch_shapes=[
+                pltpu.VMEM((MOVE, w[0].shape[1] // CUTS, C), bf),
+                pltpu.VMEM((MOVE, w[2].shape[1] // CUTS, CD), bf),
+                dma((max(len(still), 1),)),
+                dma((MOVE,)),
+                dma((MOVE,)),
+            ],
+            input_output_aliases={begin + i: to for i, to in enumerate(where)},
             compiler_params=local,
-            cost_estimate=cost(4 * w[k].size),
-        )(pltpu.with_memory_space_constraint(got[k], pltpu.HBM))
+            cost_estimate=cost(4 * w[0].size),
+        )(*(pltpu.with_memory_space_constraint(x, pltpu.VMEM) for x in still),
+          *(pltpu.with_memory_space_constraint(got[k], pltpu.HBM) for k, _, _ in moved), *olds)
 
     def take(rounds, old):
         n = len(rounds)
@@ -562,23 +619,12 @@
             cost_estimate=cost(4 * n * 6 * U * 1000),
         )(old, *(got_by[r - 1] for r in rounds), *(swapped[r - 1] for r in rounds))
 
-    shapes = [x.shape for x in w[:HELD]] + [x.shape for x in (*m, *v)]
-    types = [bf] * HELD + [f32] * 6
-    placed = pl.pallas_call(
-        place_held,
-        out_shape=[jax.ShapeDtypeStruct(a, b) for a, b in zip(shapes, types, strict=True)],
-        in_specs=[vmem] * len(in_vmem),
-        out_specs=[hbm] * len(in_vmem),
-        scratch_shapes=[dma((len(in_vmem),))],
-        compiler_params=local,
-        cost_estimate=cost(8 * w[0].size),
-        name="place_held",
-    )(*in_vmem)
-    up = move(1)
-    down = move(2)
-    down = take((1, 2), down)
-    down = take((3,), down)
-    return (placed[0], up, down, *placed[1:])
+    gate, *moments = move([got[0], *got[3:9]], [])
+    (up,) = move([], [(1, pieces(1, 0, CUTS), None)])
+    down, up = move([got[2]], [(1, pieces(1, CUTS, 2 * CUTS), up)])
+    down = take(tuple(range(1, HOPS)), down)
+    down = take((HOPS,), down)
+    return (gate, up, down, *moments)
 
 
 def solution(mesh):

time: 788 us -> 811 us (1.029)
  local copies, waits for them, and re-layouts: 0 us -> 31.6 us
  Pallas kernels: 732 us -> 723 us
    unnamed x0 -> x22, local copies, waits for them, and re-layouts: none -> 31.6 us
  transfers between devices with their start and end apart: 6 -> 6, of which waited for: 1 -> 1; matrix products, arithmetic and copies ran while one was open for 0% -> 0% of each run, Pallas kernels for 6% -> 5%
where the time goes in v2:
time: 811 us; the launch traced here: 809 us
  Pallas kernels  723 us (89%)
  starting transfers between devices  40.3 us (5%)
  local copies, waits for them, and re-layouts  31.6 us (4%)
  waiting for transfers between devices  13.6 us (2%)
    pallas_call x1, Pallas kernels, step(): pl.pallas_call(functools.partial(kernel, geo), out_shape=outs, in_specs=[...  676 us
    pallas_call x3, Pallas kernels, move(): pl.pallas_call(functools.partial(place, len(still), [(p, old) for _, p, o...  40.9 us
    ppermute x3, starting transfers between devices, step(): other = lax.ppermute(seed, 'dp', [(i, i ^ 1) for i in range(2 * CHIPS)])  32.1 us
    unnamed x22, local copies, waits for them, and re-layouts  31.6 us
  transfers between devices with their start and end apart: 6, of which 1 were waited for; matrix products, arithmetic and copies ran while one was open for 0% of the time, Pallas kernels for 5%

profile of v2, /device:TPU:0, one launch (start us, length us, event | category | flops | bytes accessed | tf_op | source)
XLA Modules:
  0.0 809.3 jit_solution(11780700048875035069)
XLA Ops:
  0.6 676.4 %step.1 = (bf16[2,1152,4608]{2,1,0:T(8,128)(2,1)S(1)}, bf16[2,1152,4608]{2,1,0:T(8,128)(2,1)}, bf16[2,4608,1152]{2,1,0:T(8,128)(2,1)}, f32[2,144,4608]{2,1,0:T(8...) custom-call(bf16[1,2,1152,4608]{3,2,1,0:T(8,128)(2,1)} %refs_0_.1, ...), custom_call_target="tpu_custom_call" | custom-call | tf_op jit(solution)/shard_map/step/pallas_call | solution.py:531
  677.1 0.0 copy-start.3
  677.1 2.4 copy-done.3
  679.5 0.0 copy-start.5
  679.5 2.4 copy-done.5
  681.8 2.4 copy-done.7
  684.2 2.4 copy-done.9
  686.6 5.8 collective-permute-start
  692.4 13.6 %collective-permute-done.refs_0_ = bf16[8,64,1152]{2,1,0:T(8,128)(2,1)S(1)} collective-permute-done((bf16[8,64,1152]{2,1,0:T(8,128)(2,1)S(1)}, bf16[8,64,1152]{2,1,0:T(8,128)(2,1)S(1)}, u32[]{:S(2)}, u32[]{:S(2)}) %collective-permute-start) | collective-permute-done | bytes 1179680 | tf_op jit(solution)/shard_map/ppermute | solution.py:572
  706.0 1.7 collective-permute-start.1
  707.7 0.0 collective-permute-done.1.refs_1_
  707.7 0.7 collective-permute-start.4
  708.4 16.3 %collective-permute-start.2 = (bf16[8,64,1152]{2,1,0:T(8,128)(2,1)S(1)}, bf16[8,64,1152]{2,1,0:T(8,128)(2,1)}, u32[]{:S(2)}, u32[]{:S(2)}) collective-permute-start(bf16[8,64,1152]{2,1,0:T(8,128)(2,1)S(1)} %collective-permute-done.refs_0_), channel_id=1, source_target_pairs={{0,1},{1,0},{2,3},{3,2},{4,5},{5,4},{6,7},{7,6},{8,9},{9,8},{10,11... | collective-permute-start | bytes 3538952 | tf_op jit(solution)/shard_map/ppermute | solution.py:575
  724.7 0.1 collective-permute-start.3
  724.8 0.0 collective-permute-done.4.refs_0_
  724.8 15.7 %collective-permute-start.5 = (bf16[8,64,1152]{2,1,0:T(8,128)(2,1)S(1)}, bf16[8,64,1152]{2,1,0:T(8,128)(2,1)}, u32[]{:S(2)}, u32[]{:S(2)}) collective-permute-start(bf16[8,64,1152]{2,1,0:T(8,128)(2,1)S(1)} %collective-permute-done.4.refs_0_), channel_id=1, source_target_pairs={{0,1},{1,0},{2,3},{3,2},{4,5},{5,4},{6,7},{7,6},{8,9},{9,8},{10,11... | collective-permute-start | bytes 3538952 | tf_op jit(solution)/shard_map/ppermute | solution.py:575
  740.5 8.8 %shard_map.188.refs_2_ = bf16[2,1152,4608]{2,1,0:T(8,128)(2,1)} custom-call(bf16[2,1152,4608]{2,1,0:T(8,128)(2,1)} %get-tuple-element.37.refs_0_.refs_1_), custom_call_target="tpu_custom_call" | custom-call | flops 42467328 | bytes 42467328 | tf_op jit(solution)/shard_map/pallas_call | solution.py:591
  749.4 0.0 copy-done
  749.4 5.0 copy-done.2
  754.4 15.1 %shard_map.189 = (bf16[2,4608,1152]{2,1,0:T(8,128)(2,1)}, bf16[2,1152,4608]{2,1,0:T(8,128)(2,1)}) custom-call(bf16[2,4608,1152]{2,1,0:T(8,128)(2,1)S(1)} %copy-done.2, bf16[2,1152,4608]{2,1,0:T(8,128)(2,1)} %get-tuple-element.37.refs_0_.refs_1_, bf16[2,1152,4608]{2,1,0:T(8,128)(2,1)} %shard_map.188.refs_2_), custom_call_target="tpu_custom_call", output_to_operand_aliasing={{1}: (2, {})} | custom-call | flops 42467328 | bytes 42467328 | tf_op jit(solution)/shard_map/pallas_call | solution.py:591
  769.5 0.0 copy-start.1
  769.5 7.0 copy-done.1
  776.5 2.5 copy-done.4
  779.0 2.5 copy-done.6
  781.5 2.5 copy-done.8
  784.0 2.5 copy-done.10
  786.5 17.0 %shard_map.187 = (bf16[2,1152,4608]{2,1,0:T(8,128)(2,1)}, f32[2,144,4608]{2,1,0:T(8,128)}, f32[2,144,4608]{2,1,0:T(8,128)}, f32[2,576,1152]{2,1,0:T(8,128)}, f32...) custom-call(bf16[2,1152,4608]{2,1,0:T(8,128)(2,1)S(1)} %copy-done.1, ...), custom_call_target="tpu_custom_call" | custom-call | flops 42467328 | bytes 42467328 | tf_op jit(solution)/shard_map/pallas_call | solution.py:591
  803.6 0.0 collective-permute-done.2.refs_2_
  803.6 0.0 collective-permute-done.3.refs_3_
  803.6 3.4 shard_map.190.old
  807.0 0.0 collective-permute-done.5.refs_1_
  807.0 2.3 shard_map.191
  (8 shorter events, 0.0 us)
Async XLA Ops:
  677.1 2.4 copy-start.3
  679.5 2.4 copy-start.5
  681.8 2.4 copy-start.7
  684.2 2.4 copy-start.9
  686.6 62.8 %copy-start = (bf16[2,1152,4608]{2,1,0:T(8,128)(2,1)}, bf16[2,1152,4608]{2,1,0:T(8,128)(2,1)S(1)}, u32[]{:S(2)}) copy-start(bf16[2,1152,4608]{2,1,0:T(8,128)(2,1)S(1)} %get-tuple-element.28.refs_0_) | copy-start | bytes 63700996
  686.6 19.4 %collective-permute-start = (bf16[8,64,1152]{2,1,0:T(8,128)(2,1)S(1)}, bf16[8,64,1152]{2,1,0:T(8,128)(2,1)S(1)}, u32[]{:S(2)}, u32[]{:S(2)}) collective-permute-start(bf16[8,64,1152]{2,1,0:T(8,128)(2,1)S(1)} %get-tuple-element.40), channel_id=1, source_target_pairs={{0,2},{2,4},{4,6},{7,5},{5,3},{3,1},{8,10},{10,12},{12,14},{15,13}... | collective-permute-start | bytes 3538952 | tf_op jit(solution)/shard_map/ppermute | solution.py:572
  706.0 1.7 collective-permute-start.1
  707.7 17.1 %collective-permute-start.4 = (bf16[8,64,1152]{2,1,0:T(8,128)(2,1)}, bf16[8,64,1152]{2,1,0:T(8,128)(2,1)S(1)}, u32[]{:S(2)}, u32[]{:S(2)}) collective-permute-start(bf16[8,64,1152]{2,1,0:T(8,128)(2,1)} %collective-permute-done.1.refs_1_), channel_id=1, source_target_pairs={{4,6},{3,1},{12,14},{11,9},{20,22},{19,17},{28,30},{27,25}} | collective-permute-start | bytes 3538952 | tf_op jit(solution)/shard_map/ppermute | solution.py:572
  708.4 95.1 %collective-permute-start.2 = (bf16[8,64,1152]{2,1,0:T(8,128)(2,1)S(1)}, bf16[8,64,1152]{2,1,0:T(8,128)(2,1)}, u32[]{:S(2)}, u32[]{:S(2)}) collective-permute-start(bf16[8,64,1152]{2,1,0:T(8,128)(2,1)S(1)} %collective-permute-done.refs_0_), channel_id=1, source_target_pairs={{0,1},{1,0},{2,3},{3,2},{4,5},{5,4},{6,7},{7,6},{8,9},{9,8},{10,11... | collective-permute-start | bytes 3538952 | tf_op jit(solution)/shard_map/ppermute | solution.py:575
  724.7 78.8 %collective-permute-start.3 = (bf16[8,64,1152]{2,1,0:T(8,128)(2,1)}, bf16[8,64,1152]{2,1,0:T(8,128)(2,1)}, u32[]{:S(2)}, u32[]{:S(2)}) collective-permute-start(bf16[8,64,1152]{2,1,0:T(8,128)(2,1)} %collective-permute-done.1.refs_1_), channel_id=1, source_target_pairs={{0,1},{1,0},{2,3},{3,2},{4,5},{5,4},{6,7},{7,6},{8,9},{9,8},{10,11... | collective-permute-start | bytes 3538952 | tf_op jit(solution)/shard_map/ppermute | solution.py:575
  724.8 82.2 %collective-permute-start.5 = (bf16[8,64,1152]{2,1,0:T(8,128)(2,1)S(1)}, bf16[8,64,1152]{2,1,0:T(8,128)(2,1)}, u32[]{:S(2)}, u32[]{:S(2)}) collective-permute-start(bf16[8,64,1152]{2,1,0:T(8,128)(2,1)S(1)} %collective-permute-done.4.refs_0_), channel_id=1, source_target_pairs={{0,1},{1,0},{2,3},{3,2},{4,5},{5,4},{6,7},{7,6},{8,9},{9,8},{10,11... | collective-permute-start | bytes 3538952 | tf_op jit(solution)/shard_map/ppermute | solution.py:575
  740.5 13.9 %copy-start.2 = (bf16[2,4608,1152]{2,1,0:T(8,128)(2,1)S(1)}, bf16[2,4608,1152]{2,1,0:T(8,128)(2,1)}, u32[]{:S(2)}) copy-start(bf16[2,4608,1152]{2,1,0:T(8,128)(2,1)} %get-tuple-element.36.refs_0_) | copy-start | bytes 63700996
  769.5 7.0 copy-start.1
  776.5 2.5 copy-start.4
  779.0 2.5 copy-start.6
  781.5 2.5 copy-start.8
  784.0 2.5 copy-start.10

commit v3 on v2

--- a/solution.py
+++ b/solution.py
@@ -21,6 +21,7 @@
 RING = 3
 FR = 2
 CUTS = 24
+SPLIT = 26
 MOVE = 8
 U = 4
 HOPS = CHIPS - 1
@@ -619,12 +620,12 @@
             cost_estimate=cost(4 * n * 6 * U * 1000),
         )(old, *(got_by[r - 1] for r in rounds), *(swapped[r - 1] for r in rounds))
 
-    gate, *moments = move([got[0], *got[3:9]], [])
-    (up,) = move([], [(1, pieces(1, 0, CUTS), None)])
-    down, up = move([got[2]], [(1, pieces(1, CUTS, 2 * CUTS), up)])
+    gate, *moments = move([got[0], *got[3:8]], [])
+    last, up = move(got[8:9], [(1, pieces(1, 0, SPLIT), None)])
+    down, up = move([got[2]], [(1, pieces(1, SPLIT, 2 * CUTS), up)])
     down = take(tuple(range(1, HOPS)), down)
     down = take((HOPS,), down)
-    return (gate, up, down, *moments)
+    return (gate, up, down, *moments, last)
 
 
 def solution(mesh):

time: 811 us -> 807 us (level)
  local copies, waits for them, and re-layouts: 31.6 us -> 21.9 us
    unnamed x22 -> x16, local copies, waits for them, and re-layouts: 31.6 us -> 21.9 us
  transfers between devices with their start and end apart: 6 -> 6, of which waited for: 1 -> 1; matrix products, arithmetic and copies ran while one was open for 0% -> 0% of each run, Pallas kernels for 5% -> 6%
where the time goes in v3:
time: 807 us; the launch traced here: 806 us
  Pallas kernels  729 us (90%)
  starting transfers between devices  40.3 us (5%)
  local copies, waits for them, and re-layouts  21.9 us (3%)
  waiting for transfers between devices  13.6 us (2%)
    pallas_call x1, Pallas kernels, step(): pl.pallas_call(functools.partial(kernel, geo), out_shape=outs, in_specs=[...  676 us
    pallas_call x3, Pallas kernels, move(): pl.pallas_call(functools.partial(place, len(still), [(p, old) for _, p, o...  47 us
    ppermute x3, starting transfers between devices, step(): other = lax.ppermute(seed, 'dp', [(i, i ^ 1) for i in range(2 * CHIPS)])  32.1 us
    unnamed x16, local copies, waits for them, and re-layouts  21.9 us
  transfers between devices with their start and end apart: 6, of which 1 were waited for; matrix products, arithmetic and copies ran while one was open for 0% of the time, Pallas kernels for 6%

profile of v3, /device:TPU:0, one launch (start us, length us, event | category | flops | bytes accessed | tf_op | source)
XLA Modules:
  0.0 805.7 jit_solution(16096493859689432676)
XLA Ops:
  0.6 676.4 %step.1 = (bf16[2,1152,4608]{2,1,0:T(8,128)(2,1)S(1)}, bf16[2,1152,4608]{2,1,0:T(8,128)(2,1)}, bf16[2,4608,1152]{2,1,0:T(8,128)(2,1)}, f32[2,144,4608]{2,1,0:T(8...) custom-call(bf16[1,2,1152,4608]{3,2,1,0:T(8,128)(2,1)} %refs_0_.1, ...), custom_call_target="tpu_custom_call" | custom-call | tf_op jit(solution)/shard_map/step/pallas_call | solution.py:532
  677.1 0.0 copy-start
  677.1 7.6 copy-done
  684.7 0.0 copy-start.3
  684.7 2.4 copy-done.3
  687.1 0.0 copy-start.4
  687.1 2.4 copy-done.4
  689.5 5.8 collective-permute-start
  695.2 13.6 %collective-permute-done.refs_0_ = bf16[8,64,1152]{2,1,0:T(8,128)(2,1)S(1)} collective-permute-done((bf16[8,64,1152]{2,1,0:T(8,128)(2,1)S(1)}, bf16[8,64,1152]{2,1,0:T(8,128)(2,1)S(1)}, u32[]{:S(2)}, u32[]{:S(2)}) %collective-permute-start) | collective-permute-done | bytes 1179680 | tf_op jit(solution)/shard_map/ppermute | solution.py:573
  708.9 1.7 collective-permute-start.1
  710.6 0.0 collective-permute-done.1.refs_1_
  710.6 0.7 collective-permute-start.4
  711.3 16.3 %collective-permute-start.2 = (bf16[8,64,1152]{2,1,0:T(8,128)(2,1)S(1)}, bf16[8,64,1152]{2,1,0:T(8,128)(2,1)}, u32[]{:S(2)}, u32[]{:S(2)}) collective-permute-start(bf16[8,64,1152]{2,1,0:T(8,128)(2,1)S(1)} %collective-permute-done.refs_0_), channel_id=1, source_target_pairs={{0,1},{1,0},{2,3},{3,2},{4,5},{5,4},{6,7},{7,6},{8,9},{9,8},{10,11... | collective-permute-start | bytes 3538952 | tf_op jit(solution)/shard_map/ppermute | solution.py:576
  727.6 0.1 collective-permute-start.3
  727.7 0.0 collective-permute-done.4.refs_0_
  727.7 15.7 %collective-permute-start.5 = (bf16[8,64,1152]{2,1,0:T(8,128)(2,1)S(1)}, bf16[8,64,1152]{2,1,0:T(8,128)(2,1)}, u32[]{:S(2)}, u32[]{:S(2)}) collective-permute-start(bf16[8,64,1152]{2,1,0:T(8,128)(2,1)S(1)} %collective-permute-done.4.refs_0_), channel_id=1, source_target_pairs={{0,1},{1,0},{2,3},{3,2},{4,5},{5,4},{6,7},{7,6},{8,9},{9,8},{10,11... | collective-permute-start | bytes 3538952 | tf_op jit(solution)/shard_map/ppermute | solution.py:576
  743.4 0.0 copy-start.5
  743.4 2.5 copy-done.5
  745.9 17.0 %shard_map.188 = (f32[2,576,1152]{2,1,0:T(8,128)}, bf16[2,1152,4608]{2,1,0:T(8,128)(2,1)}) custom-call(f32[2,576,1152]{2,1,0:T(8,128)S(1)} %copy-done.5, bf16[2,1152,4608]{2,1,0:T(8,128)(2,1)} %get-tuple-element.37.refs_1_), custom_call_target="tpu_custom_call" | custom-call | flops 42467328 | bytes 42467328 | tf_op jit(solution)/shard_map/pallas_call | solution.py:592
  762.9 0.0 copy-done.2
  762.9 0.0 slice-start.1
  762.9 14.5 %shard_map.189 = (bf16[2,4608,1152]{2,1,0:T(8,128)(2,1)}, bf16[2,1152,4608]{2,1,0:T(8,128)(2,1)}) custom-call(bf16[2,4608,1152]{2,1,0:T(8,128)(2,1)S(1)} %copy-done.2, bf16[2,1152,4608]{2,1,0:T(8,128)(2,1)} %get-tuple-element.37.refs_1_, bf16[2,1152,4608]{2,1,0:T(8,128)(2,1)} %get-tuple-element.39.refs_2_), custom_call_target="tpu_custom_call", output_to_operand_aliasing={{1}: (2, {})} | custom-call | flops 42467328 | bytes 42467328 | tf_op jit(solution)/shard_map/pallas_call | solution.py:592
  777.5 0.0 slice-done
  777.5 0.0 slice-done.1
  777.5 0.0 copy-start.1
  777.5 7.0 copy-done.1
  784.6 15.4 %shard_map.187 = (bf16[2,1152,4608]{2,1,0:T(8,128)(2,1)}, f32[2,144,4608]{2,1,0:T(8,128)}, f32[2,144,4608]{2,1,0:T(8,128)}, f32[2,576,1152]{2,1,0:T(8,128)}, f32...) custom-call(bf16[2,1152,4608]{2,1,0:T(8,128)(2,1)S(1)} %copy-done.1, f32[2,144,4608]{2,1,0:T(8,128)S(1)} %bitcast.1, ...), custom_call_target="tpu_custom_call" | custom-call | flops 42467328 | bytes 42467328 | tf_op jit(solution)/shard_map/pallas_call | solution.py:592
  800.0 0.0 collective-permute-done.2.refs_2_
  800.0 0.0 collective-permute-done.3.refs_3_
  800.0 3.4 shard_map.190.old
  803.4 0.0 collective-permute-done.5.refs_1_
  803.4 2.3 shard_map.191
  (3 shorter events, 0.0 us)
Async XLA Ops:
  677.1 7.6 copy-start
  684.7 2.4 copy-start.3
  687.1 2.4 copy-start.4
  689.5 19.4 %collective-permute-start = (bf16[8,64,1152]{2,1,0:T(8,128)(2,1)S(1)}, bf16[8,64,1152]{2,1,0:T(8,128)(2,1)S(1)}, u32[]{:S(2)}, u32[]{:S(2)}) collective-permute-start(bf16[8,64,1152]{2,1,0:T(8,128)(2,1)S(1)} %get-tuple-element.42), channel_id=1, source_target_pairs={{0,2},{2,4},{4,6},{7,5},{5,3},{3,1},{8,10},{10,12},{12,14},{15,13}... | collective-permute-start | bytes 3538952 | tf_op jit(solution)/shard_map/ppermute | solution.py:573
  708.9 1.7 collective-permute-start.1
  710.6 17.1 %collective-permute-start.4 = (bf16[8,64,1152]{2,1,0:T(8,128)(2,1)}, bf16[8,64,1152]{2,1,0:T(8,128)(2,1)S(1)}, u32[]{:S(2)}, u32[]{:S(2)}) collective-permute-start(bf16[8,64,1152]{2,1,0:T(8,128)(2,1)} %collective-permute-done.1.refs_1_), channel_id=1, source_target_pairs={{4,6},{3,1},{12,14},{11,9},{20,22},{19,17},{28,30},{27,25}} | collective-permute-start | bytes 3538952 | tf_op jit(solution)/shard_map/ppermute | solution.py:573
  711.3 88.7 %collective-permute-start.2 = (bf16[8,64,1152]{2,1,0:T(8,128)(2,1)S(1)}, bf16[8,64,1152]{2,1,0:T(8,128)(2,1)}, u32[]{:S(2)}, u32[]{:S(2)}) collective-permute-start(bf16[8,64,1152]{2,1,0:T(8,128)(2,1)S(1)} %collective-permute-done.refs_0_), channel_id=1, source_target_pairs={{0,1},{1,0},{2,3},{3,2},{4,5},{5,4},{6,7},{7,6},{8,9},{9,8},{10,11... | collective-permute-start | bytes 3538952 | tf_op jit(solution)/shard_map/ppermute | solution.py:576
  727.6 72.4 %collective-permute-start.3 = (bf16[8,64,1152]{2,1,0:T(8,128)(2,1)}, bf16[8,64,1152]{2,1,0:T(8,128)(2,1)}, u32[]{:S(2)}, u32[]{:S(2)}) collective-permute-start(bf16[8,64,1152]{2,1,0:T(8,128)(2,1)} %collective-permute-done.1.refs_1_), channel_id=1, source_target_pairs={{0,1},{1,0},{2,3},{3,2},{4,5},{5,4},{6,7},{7,6},{8,9},{9,8},{10,11... | collective-permute-start | bytes 3538952 | tf_op jit(solution)/shard_map/ppermute | solution.py:576
  727.7 75.7 %collective-permute-start.5 = (bf16[8,64,1152]{2,1,0:T(8,128)(2,1)S(1)}, bf16[8,64,1152]{2,1,0:T(8,128)(2,1)}, u32[]{:S(2)}, u32[]{:S(2)}) collective-permute-start(bf16[8,64,1152]{2,1,0:T(8,128)(2,1)S(1)} %collective-permute-done.4.refs_0_), channel_id=1, source_target_pairs={{0,1},{1,0},{2,3},{3,2},{4,5},{5,4},{6,7},{7,6},{8,9},{9,8},{10,11... | collective-permute-start | bytes 3538952 | tf_op jit(solution)/shard_map/ppermute | solution.py:576
  743.4 2.5 copy-start.5
  745.9 17.0 %copy-start.2 = (bf16[2,4608,1152]{2,1,0:T(8,128)(2,1)S(1)}, bf16[2,4608,1152]{2,1,0:T(8,128)(2,1)}, u32[]{:S(2)}) copy-start(bf16[2,4608,1152]{2,1,0:T(8,128)(2,1)} %get-tuple-element.36.refs_0_) | copy-start | bytes 63700996
  745.9 31.6 %slice-start = ((s8[5308416]{0:T(1024)(128)(4,1)}), s8[4194304]{0:T(1024)(128)(4,1)S(1)}, s32[]{:S(2)}) async-start(s8[5308416]{0:T(1024)(128)(4,1)} %bitcast), calls=%async_computation | async-start | bytes 8388608
  762.9 14.6 %slice-start.1 = ((s8[5308416]{0:T(1024)(128)(4,1)}), s8[1114112]{0:T(1024)(128)(4,1)S(1)}, s32[]{:S(2)}) async-start(s8[5308416]{0:T(1024)(128)(4,1)} %bitcast), calls=%async_computation.1 | async-start | bytes 2228224
  777.5 7.0 copy-start.1

commit v4 on v3

--- a/solution.py
+++ b/solution.py
@@ -20,10 +20,10 @@
 PF = 2
 RING = 3
 FR = 2
-CUTS = 24
-SPLIT = 26
-MOVE = 8
-U = 4
+CUTS = 12
+SPLIT = 13
+MOVE = 10
+U = (4, 3)
 HOPS = CHIPS - 1
 VMEM_LIMIT = 10 << 20
 HELD = 1
@@ -220,8 +220,9 @@
     def handle(d, t):
         q = qs[d]
         e = t - LAG * q - jnp.where(q == CHIPS - 1, END, 0)
-        sent = NC - (q + 1) * U
-        came = jnp.where(q == 0, sent, sent + U)
+        count = jnp.where(c == 0, U[0], U[1])
+        sent = NC - (q + 1) * count
+        came = jnp.where(q == 0, sent, sent + count)
         valid = (e >= 0) & (e < 3 * NC + came)
         beta, j = decode(e)
         b = beta if d == 0 else CHIPS - 1 - beta
@@ -344,10 +345,10 @@
 
         i = jnp.where(q == 0, j, j - sent)
 
-        @pl.when(valid & (beta == 0) & (q < CHIPS - 1) & (i >= 0) & (i < U))
+        @pl.when(valid & (beta == 0) & (q < CHIPS - 1) & (i >= 0) & (i < count))
         def _():
             _, l, r = split(sent + i)
-            src, dst = weight(2, l, dev, r), seed.at[c * U + i]
+            src, dst = weight(2, l, dev, r), seed.at[c * U[0] + i]
 
             @pl.when(c == d)
             def _():
@@ -408,33 +409,37 @@
         for d in range(2):
             wait_local(par.at[d, e], d2d_first.at[d, e])
 
-    def pushed(k, l, chunks):
+    def pushed(k, l, sem, chunks):
         if chunks:
             n = chunks * (ROWS if k < 2 else ROWS * R)
-            for sem in (ag_send, ag_recv):
-                pltpu.make_async_copy(W[k].at[l, pl.ds(0, n), :], W[k].at[l, pl.ds(0, n), :], sem.at[k * LAYERS + l]).wait()
+            some = W[k].at[l, pl.ds(0, n), :]
+            pltpu.make_async_copy(some, some, sem.at[k * LAYERS + l]).wait()
 
     for k in range(2):
         for l in range(LAYERS):
-            pushed(k, l, CHIPS * NR)
+            for sem in (ag_send, ag_recv):
+                pushed(k, l, sem, CHIPS * NR)
     for at in range(CHIPS):
-        @pl.when(z == at)
-        def _(at=at):
-            for l in range(LAYERS):
-                start = (2 * LAYERS + l) * NR
-                here = [NC - far * U for far in (at, CHIPS - 1 - at)]
-                pushed(2, l, 2 * NR + sum(min(max(n - start, 0), NR) for n in here))
-
-    lane = seed.at[pl.ds(0, U)]
+        for mine in range(2):
+            @pl.when((z == at) & (c == mine))
+            def _(at=at, mine=mine):
+                for sem, lane in ((ag_send, mine), (ag_recv, 1 - mine)):
+                    here = [NC - far * U[lane] for far in (at, CHIPS - 1 - at)]
+                    for l in range(LAYERS):
+                        start = (2 * LAYERS + l) * NR
+                        pushed(2, l, sem, 2 * NR + sum(min(max(n - start, 0), NR) for n in here))
+
     for d in range(2):
+        own_lane, other_lane = seed.at[pl.ds(0, U[d])], seed.at[pl.ds(0, U[1 - d])]
+
         @pl.when((c == d) & (qs[d] < CHIPS - 1))
-        def _():
-            wait_local(lane, seed_sem.at[0])
-            wait_local(lane, seed_sem.at[2])
+        def _(own_lane=own_lane, other_lane=other_lane):
+            wait_local(own_lane, seed_sem.at[0])
+            wait_local(other_lane, seed_sem.at[2])
 
         @pl.when((c != d) & (qs[d] < CHIPS - 1))
-        def _():
-            wait_local(lane, seed_sem.at[1])
+        def _(other_lane=other_lane):
+            wait_local(other_lane, seed_sem.at[1])
 
 
 def place(still, moved, *refs):
@@ -497,14 +502,14 @@
 
     def put(a, r, d, sem):
         for lane in range(2):
-            for i in range(U):
-                j = NC - qs[d] * U + (r - 1) * U + i - 2 * LAYERS * NR
+            for i in range(U[lane]):
+                j = NC - qs[d] * U[lane] + (r - 1) * U[lane] + i - 2 * LAYERS * NR
                 block = (0 if d == 0 else CHIPS - 1) * 2 + lane
                 to = new.at[j // NR, pl.ds(pl.multiple_of((block * NR + j % NR) * h, h), h), :]
                 for mine, src in ((True, got[a]), (False, swapped[a])):
                     @pl.when((c == d) == mine)
                     def _(src=src, to=to, lane=lane, i=i):
-                        pltpu.make_async_copy(src.at[lane * U + i], to, sem).start()
+                        pltpu.make_async_copy(src.at[lane * U[0] + i], to, sem).start()
 
     def end(a, r, d, sem):
         pltpu.make_async_copy(got[a], got[a], sem).wait()
@@ -525,7 +530,7 @@
     hbm, vmem = pl.BlockSpec(memory_space=pl.ANY), pl.BlockSpec(memory_space=pltpu.VMEM)
     outs = [pltpu.VMEM(x.shape, x.dtype) for x in w[:HELD]] + [jax.ShapeDtypeStruct(x.shape, x.dtype) for x in w[HELD:]]
     outs += [pltpu.VMEM(x.shape, x.dtype) for x in (*m, *v)]
-    piece = (2 * U, ROWS * (C // CD), CD)
+    piece = (sum(U), ROWS * (C // CD), CD)
     outs += [pltpu.VMEM(piece, bf)]
     outs += [jax.ShapeDtypeStruct((LAYERS, CHIPS, *x.shape[1:]), bf) for x in m]
     dma = pltpu.SemaphoreType.DMA
@@ -596,7 +601,6 @@
             out_specs=[hbm] * len(types),
             scratch_shapes=[
                 pltpu.VMEM((MOVE, w[0].shape[1] // CUTS, C), bf),
-                pltpu.VMEM((MOVE, w[2].shape[1] // CUTS, CD), bf),
                 dma((max(len(still), 1),)),
                 dma((MOVE,)),
                 dma((MOVE,)),
@@ -617,7 +621,7 @@
             scratch_shapes=[dma((2 * n,))],
             input_output_aliases={0: 0},
             compiler_params=local,
-            cost_estimate=cost(4 * n * 6 * U * 1000),
+            cost_estimate=cost(12 * n * sum(U) * 1000),
         )(old, *(got_by[r - 1] for r in rounds), *(swapped[r - 1] for r in rounds))
 
     gate, *moments = move([got[0], *got[3:8]], [])

time: 807 us -> 801 us (level)
  transfers between devices with their start and end apart: 6 -> 6, of which waited for: 1 -> 1; matrix products, arithmetic and copies ran while one was open for 0% -> 0% of each run, Pallas kernels for 6% -> 5%
where the time goes in v4:
time: 801 us; the launch traced here: 800 us
  Pallas kernels  721 us (90%)
  starting transfers between devices  37.7 us (5%)
  local copies, waits for them, and re-layouts  27.6 us (3%)
  waiting for transfers between devices  12.1 us (2%)
    pallas_call x1, Pallas kernels, step(): pl.pallas_call(functools.partial(kernel, geo), out_shape=outs, in_specs=[...  676 us
    pallas_call x3, Pallas kernels, move(): pl.pallas_call(functools.partial(place, len(still), [(p, old) for _, p, o...  39.9 us
    ppermute x3, starting transfers between devices, step(): other = lax.ppermute(seed, 'dp', [(i, i ^ 1) for i in range(2 * CHIPS)])  29.3 us
    unnamed x16, local copies, waits for them, and re-layouts  27.6 us
  transfers between devices with their start and end apart: 6, of which 1 were waited for; matrix products, arithmetic and copies ran while one was open for 0% of the time, Pallas kernels for 5%

profile of v4, /device:TPU:0, one launch (start us, length us, event | category | flops | bytes accessed | tf_op | source)
XLA Modules:
  0.0 799.6 jit_solution(1643235131019475205)
XLA Ops:
  0.6 676.5 %step.1 = (bf16[2,1152,4608]{2,1,0:T(8,128)(2,1)S(1)}, bf16[2,1152,4608]{2,1,0:T(8,128)(2,1)}, bf16[2,4608,1152]{2,1,0:T(8,128)(2,1)}, f32[2,144,4608]{2,1,0:T(8...) custom-call(bf16[1,2,1152,4608]{3,2,1,0:T(8,128)(2,1)} %refs_0_.1, ...), custom_call_target="tpu_custom_call" | custom-call | tf_op jit(solution)/shard_map/step/pallas_call | solution.py:537
  677.1 0.0 copy-start
  677.1 7.6 copy-done
  684.7 0.0 copy-start.3
  684.7 2.4 copy-done.3
  687.1 0.0 copy-start.4
  687.1 2.4 copy-done.4
  689.5 7.0 collective-permute-start
  696.5 12.1 %collective-permute-done.refs_0_ = bf16[7,64,1152]{2,1,0:T(8,128)(2,1)S(1)} collective-permute-done((bf16[7,64,1152]{2,1,0:T(8,128)(2,1)S(1)}, bf16[7,64,1152]{2,1,0:T(8,128)(2,1)S(1)}, u32[]{:S(2)}, u32[]{:S(2)}) %collective-permute-start) | collective-permute-done | bytes 1032224 | tf_op jit(solution)/shard_map/ppermute | solution.py:578
  708.6 0.7 collective-permute-start.1
  709.3 0.0 collective-permute-done.1.refs_1_
  709.3 0.7 collective-permute-start.4
  710.1 15.3 %collective-permute-start.2 = (bf16[7,64,1152]{2,1,0:T(8,128)(2,1)S(1)}, bf16[7,64,1152]{2,1,0:T(8,128)(2,1)}, u32[]{:S(2)}, u32[]{:S(2)}) collective-permute-start(bf16[7,64,1152]{2,1,0:T(8,128)(2,1)S(1)} %collective-permute-done.refs_0_), channel_id=1, source_target_pairs={{0,1},{1,0},{2,3},{3,2},{4,5},{5,4},{6,7},{7,6},{8,9},{9,8},{10,11... | collective-permute-start | bytes 3096584 | tf_op jit(solution)/shard_map/ppermute | solution.py:581
  725.3 0.1 collective-permute-start.3
  725.4 0.0 collective-permute-done.4.refs_0_
  725.4 13.9 %collective-permute-start.5 = (bf16[7,64,1152]{2,1,0:T(8,128)(2,1)S(1)}, bf16[7,64,1152]{2,1,0:T(8,128)(2,1)}, u32[]{:S(2)}, u32[]{:S(2)}) collective-permute-start(bf16[7,64,1152]{2,1,0:T(8,128)(2,1)S(1)} %collective-permute-done.4.refs_0_), channel_id=1, source_target_pairs={{0,1},{1,0},{2,3},{3,2},{4,5},{5,4},{6,7},{7,6},{8,9},{9,8},{10,11... | collective-permute-start | bytes 3096584 | tf_op jit(solution)/shard_map/ppermute | solution.py:581
  739.3 0.0 copy-start.5
  739.3 2.5 copy-done.5
  741.8 0.0 copy-start.2
  741.8 10.6 %shard_map.188 = (f32[2,576,1152]{2,1,0:T(8,128)}, bf16[2,1152,4608]{2,1,0:T(8,128)(2,1)}) custom-call(f32[2,576,1152]{2,1,0:T(8,128)S(1)} %copy-done.5, bf16[2,1152,4608]{2,1,0:T(8,128)(2,1)} %get-tuple-element.37.refs_1_), custom_call_target="tpu_custom_call" | custom-call | flops 42467328 | bytes 42467328 | tf_op jit(solution)/shard_map/pallas_call | solution.py:597
  752.5 5.7 copy-done.2
  758.2 13.8 %shard_map.189 = (bf16[2,4608,1152]{2,1,0:T(8,128)(2,1)}, bf16[2,1152,4608]{2,1,0:T(8,128)(2,1)}) custom-call(bf16[2,4608,1152]{2,1,0:T(8,128)(2,1)S(1)} %copy-done.2, bf16[2,1152,4608]{2,1,0:T(8,128)(2,1)} %get-tuple-element.37.refs_1_, bf16[2,1152,4608]{2,1,0:T(8,128)(2,1)} %get-tuple-element.39.refs_2_), custom_call_target="tpu_custom_call", output_to_operand_aliasing={{1}: (2, {})} | custom-call | flops 42467328 | bytes 42467328 | tf_op jit(solution)/shard_map/pallas_call | solution.py:597
  772.0 0.0 slice-done
  772.0 0.0 slice-done.1
  772.0 0.0 copy-start.1
  772.0 7.0 copy-done.1
  779.1 15.4 %shard_map.187 = (bf16[2,1152,4608]{2,1,0:T(8,128)(2,1)}, f32[2,144,4608]{2,1,0:T(8,128)}, f32[2,144,4608]{2,1,0:T(8,128)}, f32[2,576,1152]{2,1,0:T(8,128)}, f32...) custom-call(bf16[2,1152,4608]{2,1,0:T(8,128)(2,1)S(1)} %copy-done.1, f32[2,144,4608]{2,1,0:T(8,128)S(1)} %bitcast.1, ...), custom_call_target="tpu_custom_call" | custom-call | flops 42467328 | bytes 42467328 | tf_op jit(solution)/shard_map/pallas_call | solution.py:597
  794.5 0.0 collective-permute-done.2.refs_2_
  794.5 0.0 collective-permute-done.3.refs_3_
  794.6 2.9 shard_map.190.old
  797.4 0.0 collective-permute-done.5.refs_1_
  797.4 2.2 shard_map.191
  (3 shorter events, 0.0 us)
Async XLA Ops:
  677.1 7.6 copy-start
  684.7 2.4 copy-start.3
  687.1 2.4 copy-start.4
  689.5 19.1 %collective-permute-start = (bf16[7,64,1152]{2,1,0:T(8,128)(2,1)S(1)}, bf16[7,64,1152]{2,1,0:T(8,128)(2,1)S(1)}, u32[]{:S(2)}, u32[]{:S(2)}) collective-permute-start(bf16[7,64,1152]{2,1,0:T(8,128)(2,1)S(1)} %get-tuple-element.42), channel_id=1, source_target_pairs={{0,2},{2,4},{4,6},{7,5},{5,3},{3,1},{8,10},{10,12},{12,14},{15,13}... | collective-permute-start | bytes 3096584 | tf_op jit(solution)/shard_map/ppermute | solution.py:578
  708.6 0.7 collective-permute-start.1
  709.3 16.1 %collective-permute-start.4 = (bf16[7,64,1152]{2,1,0:T(8,128)(2,1)S(1)}, bf16[7,64,1152]{2,1,0:T(8,128)(2,1)S(1)}, u32[]{:S(2)}, u32[]{:S(2)}) collective-permute-start(bf16[7,64,1152]{2,1,0:T(8,128)(2,1)S(1)} %collective-permute-done.1.refs_1_), channel_id=1, source_target_pairs={{4,6},{3,1},{12,14},{11,9},{20,22},{19,17},{28,30},{27,25}} | collective-permute-start | bytes 3096584 | tf_op jit(solution)/shard_map/ppermute | solution.py:578
  710.1 84.5 %collective-permute-start.2 = (bf16[7,64,1152]{2,1,0:T(8,128)(2,1)S(1)}, bf16[7,64,1152]{2,1,0:T(8,128)(2,1)}, u32[]{:S(2)}, u32[]{:S(2)}) collective-permute-start(bf16[7,64,1152]{2,1,0:T(8,128)(2,1)S(1)} %collective-permute-done.refs_0_), channel_id=1, source_target_pairs={{0,1},{1,0},{2,3},{3,2},{4,5},{5,4},{6,7},{7,6},{8,9},{9,8},{10,11... | collective-permute-start | bytes 3096584 | tf_op jit(solution)/shard_map/ppermute | solution.py:581
  725.3 69.2 %collective-permute-start.3 = (bf16[7,64,1152]{2,1,0:T(8,128)(2,1)S(1)}, bf16[7,64,1152]{2,1,0:T(8,128)(2,1)}, u32[]{:S(2)}, u32[]{:S(2)}) collective-permute-start(bf16[7,64,1152]{2,1,0:T(8,128)(2,1)S(1)} %collective-permute-done.1.refs_1_), channel_id=1, source_target_pairs={{0,1},{1,0},{2,3},{3,2},{4,5},{5,4},{6,7},{7,6},{8,9},{9,8},{10,11... | collective-permute-start | bytes 3096584 | tf_op jit(solution)/shard_map/ppermute | solution.py:581
  725.4 72.0 %collective-permute-start.5 = (bf16[7,64,1152]{2,1,0:T(8,128)(2,1)S(1)}, bf16[7,64,1152]{2,1,0:T(8,128)(2,1)}, u32[]{:S(2)}, u32[]{:S(2)}) collective-permute-start(bf16[7,64,1152]{2,1,0:T(8,128)(2,1)S(1)} %collective-permute-done.4.refs_0_), channel_id=1, source_target_pairs={{0,1},{1,0},{2,3},{3,2},{4,5},{5,4},{6,7},{7,6},{8,9},{9,8},{10,11... | collective-permute-start | bytes 3096584 | tf_op jit(solution)/shard_map/ppermute | solution.py:581
  739.3 2.5 copy-start.5
  741.8 16.3 %copy-start.2 = (bf16[2,4608,1152]{2,1,0:T(8,128)(2,1)S(1)}, bf16[2,4608,1152]{2,1,0:T(8,128)(2,1)}, u32[]{:S(2)}) copy-start(bf16[2,4608,1152]{2,1,0:T(8,128)(2,1)} %get-tuple-element.36.refs_0_) | copy-start | bytes 63700996
  741.8 30.2 %slice-start = ((s8[5308416]{0:T(1024)(128)(4,1)}), s8[4194304]{0:T(1024)(128)(4,1)S(1)}, s32[]{:S(2)}) async-start(s8[5308416]{0:T(1024)(128)(4,1)} %bitcast), calls=%async_computation | async-start | bytes 8388608
  758.2 13.9 %slice-start.1 = ((s8[5308416]{0:T(1024)(128)(4,1)}), s8[1114112]{0:T(1024)(128)(4,1)S(1)}, s32[]{:S(2)}) async-start(s8[5308416]{0:T(1024)(128)(4,1)} %bitcast), calls=%async_computation.1 | async-start | bytes 2228224
  772.0 7.0 copy-start.1
